TPU v7x, 128 devices: a whole 4x4x4 slice. The times are simulated.
128 devices in a mesh: gx: 8 (over y, core), gy: 16 (over z, x).
Axes of the slice: x: 4, y: 4, z: 4, core: 2. Of those that a mesh axis runs over, the one named last changes fastest.
Arguments:
- basis: float32 [3, 400, 8, 20480], P(None, None, 'gx', 'gy'), may hold values from -0.3125 to 0.3125
- connectivity: int32 [8, 8, 16384], P(None, 'gx', 'gy'), may hold values from 0 to 1791
- send_nodes: int32 [4, 8, 2048], P(None, 'gx', 'gy'), may hold values from 0 to 1279
- modulus: float32 [8, 16384], P('gx', 'gy'), may hold values from 0.2 to 5
- ecsw_weight: float32 [8, 16384], P('gx', 'gy'), may hold values from 0.3 to 6
- stiffness: float32 [24, 24], replicated, may hold values from -1.25 to 1.25
- coords: float32 [400], replicated, may hold values from -6 to 6
- velocity: float32 [400], replicated, may hold values from -3 to 3
- external: float32 [400], replicated, may hold values from -12 to 12
Outputs:
- final_coords: float32 [400], replicated
- final_velocity: float32 [400], replicated
- reduced_force: float32 [400], replicated
- displaced: float32 [3, 8, 20480], P(None, 'gx', 'gy')
Inputs may be any that keep to these rules, and one draw needn't show every extreme that they name: `connectivity`: entries index a partition's node table: its 1280 owned nodes, then 128 nodes from each of the neighbours below and above along gx, then below and above along gy. `send_nodes`: Owned-node indices of a partition, 128 for each neighbour, in the order below and above along gx, below and above along gy; an index may repeat.
All inputs are finite; a program needn't handle non-finite values.
Results may differ from a plain program's by a relative error of at most 0.0003.
Values sent between devices are 32-bit elements; how exact they have to be, the bound alone decides.
No kernel may reach another device: no remote copies, remote signals or barrier semaphores. Data moves between devices by JAX's collectives and lax.ppermute only.
A program may use at most 128 MiB of HBM per device.

v0:
```python
import jax
import jax.numpy as jnp
from jax import lax
from jax.sharding import Mesh
from jax.sharding import PartitionSpec as P

STEPS = 2
GX = ("gx_0", "gx_1")
GY = ("gy_0", "gy_1")
GX_GY = ("gx_0", "gx_1", "gy_0", "gy_1")


time_step = 0.05


def with_halo(x, sides, width):
    for axis, dim in sides:
        size, length = (lax.axis_size(axis), x.shape[dim])
        up = [(i, (i + 1) % size) for i in range(size - 1)]
        down = [(j, i) for i, j in up]
        last = lax.slice_in_dim(x, length - width, length, axis=dim)
        first = lax.slice_in_dim(x, 0, width, axis=dim)
        before = lax.ppermute(last, axis, up)
        after = lax.ppermute(first, axis, down)
        x = jnp.concatenate([before, x, after], axis=dim)
    return x


def one_axis_at_a_time(x, axes):
    for axis in axes:
        x = lax.psum(x, axis)
    return x


def element_forces(moved, links, stiffness, factor):
    corner = moved[:, links]
    stacked = corner.reshape(24, links.shape[1])
    strain = jnp.dot(stiffness, stacked, precision=lax.Precision.HIGHEST)
    forces = factor * (strain + strain * strain * strain / 3.0)
    return jnp.zeros_like(moved).at[:, links].add(forces.reshape(3, 8, links.shape[1]))


def trade(blocks):
    along_x = with_halo(jnp.stack([blocks[0], blocks[1]]), ((GX, 0),), 1)
    along_y = with_halo(jnp.stack([blocks[2], blocks[3]]), ((GY, 0),), 1)
    return (along_x[0], along_x[3], along_y[0], along_y[3])


def advance(partial_value, coords, velocity, external):
    reduced = one_axis_at_a_time(partial_value, GX_GY)
    velocity = velocity + time_step * (external - reduced)
    coords = coords + time_step * velocity
    return (coords, velocity, reduced)


def shards(
    basis, connectivity, send_nodes, modulus, ecsw_weight, stiffness, coords, velocity, external
):
    owned_rows = basis[:, :, 0, :]
    links = connectivity[:, 0, :]
    senders = send_nodes[:, 0, :]
    factor = (modulus * ecsw_weight)[0]
    owned_count = owned_rows.shape[2]
    margin_count = senders.shape[1]
    highest = lax.Precision.HIGHEST
    reduced = jnp.zeros_like(coords)
    for repeat in range(STEPS):
        moved_own = jnp.einsum("ckn,k->cn", owned_rows, coords, precision=highest)
        blocks = tuple((moved_own[:, senders[side]] for side in range(4)))
        moved = jnp.concatenate((moved_own,) + trade(blocks), axis=1)
        nodal = element_forces(moved, links, stiffness, factor)
        margins = tuple(
            (
                nodal[
                    :, owned_count + side * margin_count : owned_count + (side + 1) * margin_count
                ]
                for side in range(4)
            )
        )
        returned = trade(margins)
        owned_force = nodal[:, :owned_count]
        for side in range(4):
            owned_force = owned_force.at[:, senders[side]].add(returned[side])
        partial_value = jnp.einsum("ckn,cn->k", owned_rows, owned_force, precision=highest)
        coords, velocity, reduced = advance(partial_value, coords, velocity, external)
    displaced = jnp.einsum("ckn,k->cn", owned_rows, coords, precision=highest)
    return (coords, velocity, reduced, displaced[:, None, :])


def solution(mesh):
    finer = Mesh(mesh.devices.reshape(4, 2, 4, 4), ("gx_0", "gx_1", "gy_0", "gy_1"))
    return jax.shard_map(
        shards,
        mesh=finer,
        in_specs=(
            P(None, None, GX, GY),
            P(None, GX, GY),
            P(None, GX, GY),
            P(GX, GY),
            P(GX, GY),
            P(),
            P(),
            P(),
            P(),
        ),
        out_specs=(P(), P(), P(), P(None, GX, GY)),
        check_vma=False,
    )
```

profile of v0, /device:TPU:1, one launch (start us, length us, event | category | flops | bytes accessed | tf_op | source)
XLA Modules:
  0.0 326.6 jit_solution(17490678071239903637)
XLA Ops:
  0.7 0.7 fusion.48
  1.4 6.0 %fusion.8 = f32[1,3,1280]{2,0,1:T(1,128)S(1)} fusion(f32[400,1,1]{0,1,2:T(1,128)} %bitcast.207, f32[3,400,1,1280]{3,2,1,0:T(1,128)} %param.9), kind=kOutput, calls=%fused_computation.28 | convolution fusion | flops 18432000 | bytes 6160960 | tf_op jit(solution)/shard_map/ckn,k->cn/dot_general | solution.py:68
  7.4 0.3 copy.39
  7.7 0.6 gather_fusion
  8.3 4.6 %collective-permute-start = (f32[1,3,128]{1,2,0:T(8,128)S(1)}, f32[1,3,128]{1,2,0:T(8,128)S(1)}, u32[]{:S(2)}, u32[]{:S(2)}) collective-permute-start(f32[1,3,128]{1,2,0:T(8,128)S(1)} %bitcast.213), channel_id=1, source_target_pairs={{0,16},{16,32},{32,48},{48,64},{64,80},{80,96},{96,112},{1,17},{17... | collective-permute-start | bytes 4616 | tf_op jit(solution)/shard_map/ppermute | solution.py:23
  12.9 0.6 gather_fusion.1
  13.5 1.9 collective-permute-start.1
  15.5 0.6 gather_fusion.2
  16.1 3.1 collective-permute-start.2
  19.2 0.6 gather_fusion.3
  19.9 1.3 collective-permute-start.3
  21.4 3.5 %collective-permute-done.3 = f32[1,3,128]{1,2,0:T(8,128)S(1)} collective-permute-done((f32[1,3,128]{1,2,0:T(8,128)S(1)}, f32[1,3,128]{1,2,0:T(8,128)S(1)}, u32[]{:S(2)}, u32[]{:S(2)}) %collective-permute-start.3) | collective-permute-done | bytes 1568 | tf_op jit(solution)/shard_map/ppermute | solution.py:24
  24.9 27.7 %gather_fusion.4 = f32[8192,3]{1,0:T(8,128)} fusion(f32[3,1792]{0,1:T(8,128)S(1)} %bitcast_dynamic-update-slice_fusion.4, s32[8192]{0:T(1024)S(1)} %broadcast_clamp_fusion), kind=kCustom, calls=%fused_computation.4 | custom fusion | bytes 229376 | tf_op jit(solution)/shard_map/gather | solution.py:36
  52.6 2.9 copy.35
  55.5 0.2 fusion.22
  55.7 2.6 copy.36
  58.4 44.5 %scatter_custom_fusion = f32[3,1792]{0,1:T(8,128)S(1)} fusion(s32[8192]{0:T(1024)S(1)} %bitcast.201, f32[8192,3]{1,0:T(8,128)} %bitcast.189, f32[]{:T(128)} %constant.6.clone.1), kind=kCustom, calls=%fused_computation.39 | custom fusion | flops 24576 | bytes 22016 | tf_op jit(solution)/shard_map/scatter-add | solution.py:40
  102.9 5.1 %collective-permute-start.4 = (f32[1,3,128]{1,2,0:T(8,128)S(1)}, f32[1,3,128]{1,2,0:T(8,128)S(1)}, u32[]{:S(2)}, u32[]{:S(2)}) collective-permute-start(f32[1,3,128]{1,2,0:T(8,128)S(1)} %get-tuple-element.13), channel_id=1, source_target_pairs={{0,16},{16,32},{32,48},{48,64},{64,80},{80,96},{96,112},{1,17},{17... | collective-permute-start | bytes 4616 | tf_op jit(solution)/shard_map/ppermute | solution.py:23
  108.0 1.9 collective-permute-start.5
  109.9 3.1 collective-permute-start.6
  113.1 1.3 collective-permute-start.7
  114.4 1.5 scatter_custom_fusion.1
  116.0 1.5 scatter_custom_fusion.2
  117.5 1.5 scatter_custom_fusion.3
  119.0 1.7 scatter_custom_fusion.4
  120.7 0.2 copy.40
  120.9 7.8 %fusion.6 = f32[1,400,1]{1,0,2:T(1,128)S(1)} fusion(f32[3,1280,1]{1,2,0:T(1,128)S(1)} %copy.40, f32[3,400,1,1280]{3,2,1,0:T(1,128)} %param.9), kind=kOutput, calls=%fused_computation.26 | convolution fusion | flops 18432000 | bytes 6160960 | tf_op jit(solution)/shard_map/ckn,cn->k/dot_general | solution.py:84
  128.7 7.6 %psum.56 = f32[400]{0:T(512)S(1)} all-reduce(f32[400]{0:T(512)S(1)} %bitcast.209), channel_id=1, replica_groups=mesh['gx_0'=4,'gx_1'=2,'gy_0'=4,'gy_1'=4] {'gx_0'}, use_global_device_ids=true, to_apply=%region_5.0 | all-reduce | flops 400 | bytes 3200 | tf_op jit(solution)/shard_map/psum | solution.py:31
  136.2 6.3 %psum.57 = f32[400]{0:T(512)S(1)} all-reduce(f32[400]{0:T(512)S(1)} %psum.56), channel_id=1, replica_groups=mesh['gx_0'=4,'gx_1'=2,'gy_0'=4,'gy_1'=4] {'gx_1'}, use_global_device_ids=true, to_apply=%region_6.0 | all-reduce | flops 400 | bytes 3200 | tf_op jit(solution)/shard_map/psum | solution.py:31
  142.6 13.4 %psum.58 = f32[400]{0:T(512)S(1)} all-reduce(f32[400]{0:T(512)S(1)} %psum.57), channel_id=1, replica_groups=mesh['gx_0'=4,'gx_1'=2,'gy_0'=4,'gy_1'=4] {'gy_0'}, use_global_device_ids=true, to_apply=%region_7.0 | all-reduce | flops 400 | bytes 3200 | tf_op jit(solution)/shard_map/psum | solution.py:31
  156.0 6.0 %psum.59 = f32[400]{0:T(512)S(1)} all-reduce(f32[400]{0:T(512)S(1)} %psum.58), channel_id=1, replica_groups=mesh['gx_0'=4,'gx_1'=2,'gy_0'=4,'gy_1'=4] {'gy_1'}, use_global_device_ids=true, to_apply=%region_8.0 | all-reduce | flops 400 | bytes 3200 | tf_op jit(solution)/shard_map/psum | solution.py:31
  162.1 5.7 %fusion.4 = f32[1,3,1280]{2,0,1:T(1,128)S(1)} fusion(f32[400,1,1]{0,1,2:T(1,128)S(1)} %bitcast.206, f32[3,400,1,1280]{3,2,1,0:T(1,128)} %param.9), kind=kOutput, calls=%fused_computation.24 | convolution fusion | flops 18432000 | bytes 6160960 | tf_op jit(solution)/shard_map/ckn,k->cn/dot_general | solution.py:68
  167.8 0.3 copy.41
  168.0 0.6 gather_fusion.5
  168.7 5.4 %collective-permute-start.8 = (f32[1,3,128]{1,2,0:T(8,128)S(1)}, f32[1,3,128]{1,2,0:T(8,128)S(1)}, u32[]{:S(2)}, u32[]{:S(2)}) collective-permute-start(f32[1,3,128]{1,2,0:T(8,128)S(1)} %bitcast.217), channel_id=1, source_target_pairs={{0,16},{16,32},{32,48},{48,64},{64,80},{80,96},{96,112},{1,17},{17... | collective-permute-start | bytes 4616 | tf_op jit(solution)/shard_map/ppermute | solution.py:23
  174.2 0.6 gather_fusion.8
  174.8 0.6 gather_fusion.7
  175.5 0.6 gather_fusion.6
  176.1 2.1 collective-permute-start.9
  178.3 3.3 %collective-permute-start.10 = (f32[1,3,128]{1,2,0:T(8,128)S(1)}, f32[1,3,128]{1,2,0:T(8,128)S(1)}, u32[]{:S(2)}, u32[]{:S(2)}) collective-permute-start(f32[1,3,128]{1,2,0:T(8,128)S(1)} %bitcast.215), channel_id=1, source_target_pairs={{0,1},{1,2},{2,3},{3,4},{4,5},{5,6},{6,7},{7,8},{8,9},{9,10},{10,1... | collective-permute-start | bytes 4616 | tf_op jit(solution)/shard_map/ppermute | solution.py:23
  181.6 1.3 collective-permute-start.11
  182.9 0.5 collective-permute-done.10
  183.4 4.1 %collective-permute-done.11 = f32[1,3,128]{1,2,0:T(8,128)S(1)} collective-permute-done((f32[1,3,128]{1,2,0:T(8,128)S(1)}, f32[1,3,128]{1,2,0:T(8,128)S(1)}, u32[]{:S(2)}, u32[]{:S(2)}) %collective-permute-start.11) | collective-permute-done | bytes 1568 | tf_op jit(solution)/shard_map/ppermute | solution.py:24
  187.5 27.7 %gather_fusion.9 = f32[8192,3]{1,0:T(8,128)} fusion(f32[3,1792]{0,1:T(8,128)S(1)} %bitcast_dynamic-update-slice_fusion, s32[8192]{0:T(1024)S(1)} %broadcast_clamp_fusion), kind=kCustom, calls=%fused_computation.9 | custom fusion | bytes 229376 | tf_op jit(solution)/shard_map/gather | solution.py:36
  215.2 2.9 copy.37
  218.0 0.2 fusion.26
  218.2 2.6 copy.38
  220.9 44.5 %scatter_custom_fusion.5 = f32[3,1792]{0,1:T(8,128)S(1)} fusion(s32[8192]{0:T(1024)S(1)} %bitcast.202, f32[8192,3]{1,0:T(8,128)} %bitcast.188, f32[]{:T(128)} %constant.6.clone.1), kind=kCustom, calls=%fused_computation.37 | custom fusion | flops 24576 | bytes 22016 | tf_op jit(solution)/shard_map/scatter-add | solution.py:40
  265.5 4.0 %collective-permute-start.12 = (f32[1,3,128]{1,2,0:T(8,128)S(1)}, f32[1,3,128]{1,2,0:T(8,128)S(1)}, u32[]{:S(2)}, u32[]{:S(2)}) collective-permute-start(f32[1,3,128]{1,2,0:T(8,128)S(1)} %get-tuple-element.9), channel_id=1, source_target_pairs={{0,16},{16,32},{32,48},{48,64},{64,80},{80,96},{96,112},{1,17},{17... | collective-permute-start | bytes 4616 | tf_op jit(solution)/shard_map/ppermute | solution.py:23
  269.4 1.9 collective-permute-start.13
  271.4 1.6 collective-permute-start.14
  273.0 1.3 collective-permute-start.15
  274.4 1.5 scatter_custom_fusion.6
  275.9 1.5 scatter_custom_fusion.7
  277.4 1.5 scatter_custom_fusion.8
  279.0 1.7 scatter_custom_fusion.9
  280.9 7.8 %fusion.2 = f32[1,400,1]{1,0,2:T(1,128)S(1)} fusion(f32[3,1280,1]{1,2,0:T(1,128)S(1)} %copy.42, f32[3,400,1,1280]{3,2,1,0:T(1,128)} %param.9), kind=kOutput, calls=%fused_computation.22 | convolution fusion | flops 18432000 | bytes 6160960 | tf_op jit(solution)/shard_map/ckn,cn->k/dot_general | solution.py:84
  288.7 7.0 %psum.60 = f32[400]{0:T(512)S(1)} all-reduce(f32[400]{0:T(512)S(1)} %bitcast.210), channel_id=1, replica_groups=mesh['gx_0'=4,'gx_1'=2,'gy_0'=4,'gy_1'=4] {'gx_0'}, use_global_device_ids=true, to_apply=%region_14.0 | all-reduce | flops 400 | bytes 3200 | tf_op jit(solution)/shard_map/psum | solution.py:31
  295.7 5.6 %psum.61 = f32[400]{0:T(512)S(1)} all-reduce(f32[400]{0:T(512)S(1)} %psum.60), channel_id=1, replica_groups=mesh['gx_0'=4,'gx_1'=2,'gy_0'=4,'gy_1'=4] {'gx_1'}, use_global_device_ids=true, to_apply=%region_15.0 | all-reduce | flops 400 | bytes 3200 | tf_op jit(solution)/shard_map/psum | solution.py:31
  301.3 11.7 %psum.62 = f32[400]{0:T(512)S(1)} all-reduce(f32[400]{0:T(512)S(1)} %psum.61), channel_id=1, replica_groups=mesh['gx_0'=4,'gx_1'=2,'gy_0'=4,'gy_1'=4] {'gy_0'}, use_global_device_ids=true, to_apply=%region_16.0 | all-reduce | flops 400 | bytes 3200 | tf_op jit(solution)/shard_map/psum | solution.py:31
  313.0 6.6 %psum.63 = f32[400]{0:T(512)S(1)} all-reduce(f32[400]{0:T(512)S(1)} %psum.62), channel_id=1, replica_groups=mesh['gx_0'=4,'gx_1'=2,'gy_0'=4,'gy_1'=4] {'gy_1'}, use_global_device_ids=true, to_apply=%region_17.0 | all-reduce | flops 400 | bytes 3200 | tf_op jit(solution)/shard_map/psum | solution.py:31
  319.7 0.6 multiply_add_fusion
  320.3 5.7 %fusion = f32[1,3,1280]{2,0,1:T(1,128)S(1)} fusion(f32[400,1,1]{0,1,2:T(1,128)S(1)} %bitcast.208, f32[3,400,1,1280]{3,2,1,0:T(1,128)} %param.9), kind=kOutput, calls=%fused_computation.20 | convolution fusion | flops 18432000 | bytes 6160960 | tf_op jit(solution)/shard_map/ckn,k->cn/dot_general | solution.py:86
  326.0 0.6 broadcast_in_dim.2
  (53 shorter events, 0.6 us)
Async XLA Ops:
  0.6 54.8 %copy-start = (f32[24,24]{1,0:T(8,128)S(1)}, f32[24,24]{1,0:T(8,128)}, u32[]{:S(2)}) copy-start(f32[24,24]{1,0:T(8,128)} %param.14) | copy-start | bytes 6916
  0.6 20.6 %copy-start.1 = (s32[8,1,1024]{2,1,0:T(1,128)S(1)}, s32[8,1,1024]{2,1,0:T(1,128)}, u32[]{:S(2)}) copy-start(s32[8,1,1024]{2,1,0:T(1,128)} %param.10) | copy-start | bytes 98308
  0.7 20.7 %copy-start.8 = (f32[1,1024]{1,0:T(1,128)S(1)}, f32[1,1024]{1,0:T(1,128)}, u32[]{:S(2)}) copy-start(f32[1,1024]{1,0:T(1,128)} %param.13) | copy-start | bytes 12292
  0.7 20.7 %copy-start.7 = (f32[1,1024]{1,0:T(1,128)S(1)}, f32[1,1024]{1,0:T(1,128)}, u32[]{:S(2)}) copy-start(f32[1,1024]{1,0:T(1,128)} %param.12) | copy-start | bytes 12292
  8.3 13.0 %collective-permute-start = (f32[1,3,128]{1,2,0:T(8,128)S(1)}, f32[1,3,128]{1,2,0:T(8,128)S(1)}, u32[]{:S(2)}, u32[]{:S(2)}) collective-permute-start(f32[1,3,128]{1,2,0:T(8,128)S(1)} %bitcast.213), channel_id=1, source_target_pairs={{0,16},{16,32},{32,48},{48,64},{64,80},{80,96},{96,112},{1,17},{17... | collective-permute-start | bytes 4616 | tf_op jit(solution)/shard_map/ppermute | solution.py:23
  13.5 7.8 %collective-permute-start.1 = (f32[1,3,128]{1,2,0:T(8,128)S(1)}, f32[1,3,128]{1,2,0:T(8,128)S(1)}, u32[]{:S(2)}, u32[]{:S(2)}) collective-permute-start(f32[1,3,128]{1,2,0:T(8,128)S(1)} %bitcast.212), channel_id=1, source_target_pairs={{16,0},{32,16},{48,32},{64,48},{80,64},{96,80},{112,96},{17,1},{33... | collective-permute-start | bytes 4616 | tf_op jit(solution)/shard_map/ppermute | solution.py:24
  16.1 5.3 %collective-permute-start.2 = (f32[1,3,128]{1,2,0:T(8,128)S(1)}, f32[1,3,128]{1,2,0:T(8,128)S(1)}, u32[]{:S(2)}, u32[]{:S(2)}) collective-permute-start(f32[1,3,128]{1,2,0:T(8,128)S(1)} %bitcast.216), channel_id=1, source_target_pairs={{0,1},{1,2},{2,3},{3,4},{4,5},{5,6},{6,7},{7,8},{8,9},{9,10},{10,1... | collective-permute-start | bytes 4616 | tf_op jit(solution)/shard_map/ppermute | solution.py:23
  19.9 5.0 %collective-permute-start.3 = (f32[1,3,128]{1,2,0:T(8,128)S(1)}, f32[1,3,128]{1,2,0:T(8,128)S(1)}, u32[]{:S(2)}, u32[]{:S(2)}) collective-permute-start(f32[1,3,128]{1,2,0:T(8,128)S(1)} %bitcast.214), channel_id=1, source_target_pairs={{1,0},{2,1},{3,2},{4,3},{5,4},{6,5},{7,6},{8,7},{9,8},{10,9},{11,1... | collective-permute-start | bytes 4616 | tf_op jit(solution)/shard_map/ppermute | solution.py:24
  58.4 103.7 %copy-start.2 = (f32[400]{0:T(512)S(1)}, f32[400]{0:T(512)}, u32[]{:S(2)}) copy-start(f32[400]{0:T(512)} %param.15) | copy-start | bytes 4804
  58.4 103.7 %copy-start.4 = (f32[400]{0:T(512)S(1)}, f32[400]{0:T(512)}, u32[]{:S(2)}) copy-start(f32[400]{0:T(512)} %param.16) | copy-start | bytes 4804
  58.4 103.7 %copy-start.5 = (f32[400]{0:T(512)S(1)}, f32[400]{0:T(512)}, u32[]{:S(2)}) copy-start(f32[400]{0:T(512)} %param.17) | copy-start | bytes 4804
  102.9 11.5 %collective-permute-start.4 = (f32[1,3,128]{1,2,0:T(8,128)S(1)}, f32[1,3,128]{1,2,0:T(8,128)S(1)}, u32[]{:S(2)}, u32[]{:S(2)}) collective-permute-start(f32[1,3,128]{1,2,0:T(8,128)S(1)} %get-tuple-element.13), channel_id=1, source_target_pairs={{0,16},{16,32},{32,48},{48,64},{64,80},{80,96},{96,112},{1,17},{17... | collective-permute-start | bytes 4616 | tf_op jit(solution)/shard_map/ppermute | solution.py:23
  108.0 7.9 %collective-permute-start.5 = (f32[1,3,128]{1,2,0:T(8,128)S(1)}, f32[1,3,128]{1,2,0:T(8,128)S(1)}, u32[]{:S(2)}, u32[]{:S(2)}) collective-permute-start(f32[1,3,128]{1,2,0:T(8,128)S(1)} %get-tuple-element.12), channel_id=1, source_target_pairs={{16,0},{32,16},{48,32},{64,48},{80,64},{96,80},{112,96},{17,1},{33... | collective-permute-start | bytes 4616 | tf_op jit(solution)/shard_map/ppermute | solution.py:24
  109.9 7.5 %collective-permute-start.6 = (f32[1,3,128]{1,2,0:T(8,128)S(1)}, f32[1,3,128]{1,2,0:T(8,128)S(1)}, u32[]{:S(2)}, u32[]{:S(2)}) collective-permute-start(f32[1,3,128]{1,2,0:T(8,128)S(1)} %get-tuple-element.11), channel_id=1, source_target_pairs={{0,1},{1,2},{2,3},{3,4},{4,5},{5,6},{6,7},{7,8},{8,9},{9,10},{10,1... | collective-permute-start | bytes 4616 | tf_op jit(solution)/shard_map/ppermute | solution.py:23
  113.1 5.9 %collective-permute-start.7 = (f32[1,3,128]{1,2,0:T(8,128)S(1)}, f32[1,3,128]{1,2,0:T(8,128)S(1)}, u32[]{:S(2)}, u32[]{:S(2)}) collective-permute-start(f32[1,3,128]{1,2,0:T(8,128)S(1)} %get-tuple-element.10), channel_id=1, source_target_pairs={{1,0},{2,1},{3,2},{4,3},{5,4},{6,5},{7,6},{8,7},{9,8},{10,9},{11,1... | collective-permute-start | bytes 4616 | tf_op jit(solution)/shard_map/ppermute | solution.py:24
  168.7 14.2 %collective-permute-start.8 = (f32[1,3,128]{1,2,0:T(8,128)S(1)}, f32[1,3,128]{1,2,0:T(8,128)S(1)}, u32[]{:S(2)}, u32[]{:S(2)}) collective-permute-start(f32[1,3,128]{1,2,0:T(8,128)S(1)} %bitcast.217), channel_id=1, source_target_pairs={{0,16},{16,32},{32,48},{48,64},{64,80},{80,96},{96,112},{1,17},{17... | collective-permute-start | bytes 4616 | tf_op jit(solution)/shard_map/ppermute | solution.py:23
  176.1 6.8 %collective-permute-start.9 = (f32[1,3,128]{1,2,0:T(8,128)S(1)}, f32[1,3,128]{1,2,0:T(8,128)S(1)}, u32[]{:S(2)}, u32[]{:S(2)}) collective-permute-start(f32[1,3,128]{1,2,0:T(8,128)S(1)} %bitcast.218), channel_id=1, source_target_pairs={{16,0},{32,16},{48,32},{64,48},{80,64},{96,80},{112,96},{17,1},{33... | collective-permute-start | bytes 4616 | tf_op jit(solution)/shard_map/ppermute | solution.py:24
  178.3 5.1 %collective-permute-start.10 = (f32[1,3,128]{1,2,0:T(8,128)S(1)}, f32[1,3,128]{1,2,0:T(8,128)S(1)}, u32[]{:S(2)}, u32[]{:S(2)}) collective-permute-start(f32[1,3,128]{1,2,0:T(8,128)S(1)} %bitcast.215), channel_id=1, source_target_pairs={{0,1},{1,2},{2,3},{3,4},{4,5},{5,6},{6,7},{7,8},{8,9},{9,10},{10,1... | collective-permute-start | bytes 4616 | tf_op jit(solution)/shard_map/ppermute | solution.py:23
  181.6 5.9 %collective-permute-start.11 = (f32[1,3,128]{1,2,0:T(8,128)S(1)}, f32[1,3,128]{1,2,0:T(8,128)S(1)}, u32[]{:S(2)}, u32[]{:S(2)}) collective-permute-start(f32[1,3,128]{1,2,0:T(8,128)S(1)} %bitcast.211), channel_id=1, source_target_pairs={{1,0},{2,1},{3,2},{4,3},{5,4},{6,5},{7,6},{8,7},{9,8},{10,9},{11,1... | collective-permute-start | bytes 4616 | tf_op jit(solution)/shard_map/ppermute | solution.py:24
  265.5 8.9 %collective-permute-start.12 = (f32[1,3,128]{1,2,0:T(8,128)S(1)}, f32[1,3,128]{1,2,0:T(8,128)S(1)}, u32[]{:S(2)}, u32[]{:S(2)}) collective-permute-start(f32[1,3,128]{1,2,0:T(8,128)S(1)} %get-tuple-element.9), channel_id=1, source_target_pairs={{0,16},{16,32},{32,48},{48,64},{64,80},{80,96},{96,112},{1,17},{17... | collective-permute-start | bytes 4616 | tf_op jit(solution)/shard_map/ppermute | solution.py:23
  269.4 6.5 %collective-permute-start.13 = (f32[1,3,128]{1,2,0:T(8,128)S(1)}, f32[1,3,128]{1,2,0:T(8,128)S(1)}, u32[]{:S(2)}, u32[]{:S(2)}) collective-permute-start(f32[1,3,128]{1,2,0:T(8,128)S(1)} %get-tuple-element.8), channel_id=1, source_target_pairs={{16,0},{32,16},{48,32},{64,48},{80,64},{96,80},{112,96},{17,1},{33... | collective-permute-start | bytes 4616 | tf_op jit(solution)/shard_map/ppermute | solution.py:24
  271.4 6.1 %collective-permute-start.14 = (f32[1,3,128]{1,2,0:T(8,128)S(1)}, f32[1,3,128]{1,2,0:T(8,128)S(1)}, u32[]{:S(2)}, u32[]{:S(2)}) collective-permute-start(f32[1,3,128]{1,2,0:T(8,128)S(1)} %get-tuple-element.7), channel_id=1, source_target_pairs={{0,1},{1,2},{2,3},{3,4},{4,5},{5,6},{6,7},{7,8},{8,9},{9,10},{10,1... | collective-permute-start | bytes 4616 | tf_op jit(solution)/shard_map/ppermute | solution.py:23
  273.0 5.9 %collective-permute-start.15 = (f32[1,3,128]{1,2,0:T(8,128)S(1)}, f32[1,3,128]{1,2,0:T(8,128)S(1)}, u32[]{:S(2)}, u32[]{:S(2)}) collective-permute-start(f32[1,3,128]{1,2,0:T(8,128)S(1)} %get-tuple-element.6), channel_id=1, source_target_pairs={{1,0},{2,1},{3,2},{4,3},{5,4},{6,5},{7,6},{8,7},{9,8},{10,9},{11,1... | collective-permute-start | bytes 4616 | tf_op jit(solution)/shard_map/ppermute | solution.py:24
  319.7 6.9 %copy-start.6 = (f32[400]{0:T(512)}, f32[400]{0:T(512)S(1)}, u32[]{:S(2)}) copy-start(f32[400]{0:T(512)S(1)} %psum.63) | copy-start | bytes 4804
  320.3 6.3 %copy-start.3 = (f32[400]{0:T(512)}, f32[400]{0:T(512)S(1)}, u32[]{:S(2)}) copy-start(f32[400]{0:T(512)S(1)} %get-tuple-element.4) | copy-start | bytes 4804
where the time goes:
time: 330 us; the launch traced here: 327 us
  other arithmetic  103 us (31%)
  local copies, waits for them, and re-layouts  73.5 us (22%)
  blocking collectives  64.3 us (19%)
  starting transfers between devices  43.3 us (13%)
  matrix products  33.3 us (10%)
  waiting for transfers between devices  8.03 us (2%)
    scatter-add x2, other arithmetic, element_forces(): jnp.zeros_like(moved).at[:, links].add(forces.reshape(3, 8, links.shape[1]))  89.1 us
    psum x8, blocking collectives, one_axis_at_a_time(): x = lax.psum(x, axis)  64.3 us
    gather x4, local copies, waits for them, and re-layouts, element_forces(): corner = moved[:, links]  61.1 us
    ppermute x8, starting transfers between devices, with_halo(): before = lax.ppermute(last, axis, up)  30.2 us
    dot_general x2, matrix products, shards(): jnp.einsum('ckn,cn->k', owned_rows, owned_force, precision=highest)  15.5 us
    ppermute x8, starting transfers between devices, with_halo(): after = lax.ppermute(first, axis, down)  13.1 us
    scatter-add x8, other arithmetic, shards(): owned_force = owned_force.at[:, senders[side]].add(returned[side])  12.5 us
    dot_general x2, matrix products, shards(): moved_own = jnp.einsum('ckn,k->cn', owned_rows, coords, precision=highest)  11.7 us
  transfers between devices with their start and end apart: 16, of which 3 were waited for; matrix products, arithmetic and copies ran while one was open for 4% of the time, Pallas kernels for 0%

commit v1 on v0

v1 whole, which is shorter than its diff:
```python
import functools

import jax
import jax.numpy as jnp
from jax import lax
from jax.experimental import pallas as pl
from jax.experimental.pallas import tpu as pltpu
from jax.sharding import PartitionSpec as P

STEPS = 2
DT = 0.05
LANES = 128
SPLITS = 3


def lane_pick(rows, lanes):
    return jnp.take_along_axis(rows, lanes, axis=1, mode="promise_in_bounds")


def load_chunks(basis_ref, buf, sems, chunks):
    size = buf.shape[0] // chunks
    copies = []
    for i in range(chunks):
        part = pl.ds(i * size, size)
        copies.append(pltpu.make_async_copy(basis_ref.at[part], buf.at[part], sems.at[i]))
    for copy in copies:
        copy.start()
    return copies


def shared_rows_kernel(modes, tiles, chunks, basis_ref, send_ref, first_ref, second_ref, buf, sems):
    copies = load_chunks(basis_ref, buf, sems, chunks)
    outs = (first_ref, second_ref)
    picks = []
    for side in range(2):
        nodes = jnp.broadcast_to(send_ref[side : side + 1, :], (8, LANES))
        picks.append((nodes & (LANES - 1), nodes >> 7))
    groups = first_ref.shape[0] // 8 // chunks
    for i in range(chunks):
        copies[i].wait()

        def body(g, carry, i=i):
            g = g + i * groups
            sums = [jnp.zeros((8, LANES), jnp.float32) for _ in range(2)]
            for t in range(tiles):
                rows = buf[pl.ds(g * (8 * tiles) + t, 8, stride=tiles), :]
                for side in range(2):
                    lanes, tile = picks[side]
                    sums[side] = jnp.where(tile == t, lane_pick(rows, lanes), sums[side])
            for side in range(2):
                outs[side][pl.ds(pl.multiple_of(g * 8, 8), 8), :] = sums[side]
            return carry

        lax.fori_loop(0, groups, body, 0, unroll=5)


def shared_rows(basis, send, modes):
    rows = basis.shape[0]
    comps = 3
    tiles = rows // (comps * modes)
    chunks = 6
    out = jax.ShapeDtypeStruct((comps * modes, LANES), jnp.float32)
    return pl.pallas_call(
        functools.partial(shared_rows_kernel, modes, tiles, chunks),
        out_shape=(out, out),
        in_specs=[pl.BlockSpec(memory_space=pl.ANY), pl.BlockSpec(memory_space=pltpu.VMEM)],
        out_specs=(pl.BlockSpec(memory_space=pltpu.VMEM),) * 2,
        scratch_shapes=[
            pltpu.VMEM((rows, LANES), jnp.float32),
            pltpu.SemaphoreType.DMA((chunks,)),
        ],
        compiler_params=pltpu.CompilerParams(vmem_limit_bytes=16 * 2**20),
        name="shared_rows",
    )(basis, send)


def newest(first, parts_ref, coords_ref, velocity_ref, external_ref):
    coords = coords_ref[...]
    velocity = velocity_ref[...]
    if first:
        return coords, velocity, None
    reduced = jnp.sum(parts_ref[...], axis=0, keepdims=True)
    velocity = velocity + DT * (external_ref[...] - reduced)
    coords = coords + DT * velocity
    return coords, velocity, reduced


def column(row):
    return jnp.transpose(jnp.broadcast_to(row, (LANES, row.shape[1])))


def contract(buf, cols, modes, tiles, comp):
    def body(k, sums):
        scale = cols[pl.ds(pl.multiple_of(k * 8, 8), 8), :]
        base = comp * modes * tiles + k * 8 * tiles
        return tuple(
            sums[t] + buf[pl.ds(base + t, 8, stride=tiles), :] * scale for t in range(tiles)
        )

    zero = jnp.zeros((8, LANES), jnp.float32)
    sums = lax.fori_loop(0, modes // 8, body, (zero,) * tiles, unroll=5)
    return [jnp.sum(s, axis=0, keepdims=True) for s in sums]


def contract_shared(sides, cols, modes, comp):
    def body(k, sums):
        scale = cols[pl.ds(pl.multiple_of(k * 8, 8), 8), :]
        start = pl.multiple_of(comp * modes + k * 8, 8)
        return tuple(s + side[pl.ds(start, 8), :] * scale for s, side in zip(sums, sides))

    zero = jnp.zeros((8, LANES), jnp.float32)
    sums = lax.fori_loop(0, modes // 8, body, (zero,) * len(sides), unroll=5)
    return [jnp.sum(s, axis=0, keepdims=True) for s in sums]


def step_kernel(first, modes, tiles, chunks, *refs):
    if first:
        (basis_ref, r0, r1, r2, r3, links_ref, modulus_ref, weight_ref, stiff_ref,
         coords_ref, velocity_ref, external_ref, out_ref,
         buf, sems, cols, table, corner, spread, low, nodal_ref, acc_ref) = refs
        parts_ref = None
    else:
        (parts_ref, basis_ref, r0, r1, r2, r3, links_ref, modulus_ref, weight_ref, stiff_ref,
         coords_ref, velocity_ref, external_ref, out_ref, coords_out, velocity_out,
         buf, sems, cols, table, corner, spread, low, nodal_ref, acc_ref) = refs
    sides = (r0, r1, r2, r3)
    slots = tiles + len(sides)
    copies = load_chunks(basis_ref, buf, sems, chunks)
    elements = links_ref.shape[1]
    blocks = elements // LANES

    iota = lax.broadcasted_iota(jnp.int32, (LANES, LANES), 0)
    for b in range(blocks):
        for a in range(8):
            links = links_ref[a : a + 1, b * LANES : (b + 1) * LANES]
            hot = jnp.broadcast_to(links & (LANES - 1), (LANES, LANES)) == iota
            at = a * elements + b * LANES
            low[:, at : at + LANES] = jnp.where(hot, 1.0, 0.0).astype(jnp.bfloat16)

    coords, velocity, _ = newest(first, parts_ref, coords_ref, velocity_ref, external_ref)
    if not first:
        coords_out[...] = coords
        velocity_out[...] = velocity
    cols[...] = column(coords)

    per = chunks // 3
    for c in range(3):
        for i in range(per):
            copies[c * per + i].wait()
        rows = contract(buf, cols, modes, tiles, c) + contract_shared(sides, cols, modes, c)
        for r, row in enumerate(rows):
            table[c * slots + r : c * slots + r + 1, :] = row

    for b in range(blocks):
        links = links_ref[:, b * LANES : (b + 1) * LANES]
        lanes, tile = links & (LANES - 1), links >> 7
        for c in range(3):
            value = jnp.zeros((8, LANES), jnp.float32)
            for r in range(slots):
                row = jnp.broadcast_to(table[c * slots + r : c * slots + r + 1, :], (8, LANES))
                value = jnp.where(tile == r, lane_pick(row, lanes), value)
            corner[c * 8 : (c + 1) * 8, b * LANES : (b + 1) * LANES] = value

    strain = jnp.dot(
        stiff_ref[...], corner[...],
        precision=lax.Precision.HIGHEST, preferred_element_type=jnp.float32,
    )
    factor = modulus_ref[...] * weight_ref[...]
    corner[...] = factor * (strain + strain * strain * strain * (1.0 / 3.0))

    high = lax.broadcasted_iota(jnp.int32, (16, LANES), 0)
    for b in range(blocks):
        part = slice(b * LANES, (b + 1) * LANES)
        pieces = []
        rest = corner[:, part]
        for s in range(SPLITS):
            piece = rest.astype(jnp.bfloat16).astype(jnp.float32)
            pieces.append(piece)
            rest = rest - piece
        for a in range(8):
            hot = jnp.broadcast_to(links_ref[a : a + 1, part] >> 7, (16, LANES)) == high
            at = a * elements + b * LANES
            for s in range(SPLITS):
                for c in range(3):
                    row = c * 8 + a
                    value = jnp.broadcast_to(pieces[s][row : row + 1, :], (16, LANES))
                    to = (s * 3 + c) * 16
                    spread[to : to + 16, at : at + LANES] = jnp.where(hot, value, 0.0).astype(
                        jnp.bfloat16
                    )
    nodal = lax.dot_general(
        spread[...], low[...], (((1,), (1,)), ((), ())), preferred_element_type=jnp.float32
    )
    total = nodal[0:48]
    for s in range(1, SPLITS):
        total = total + nodal[s * 48 : (s + 1) * 48]
    nodal_ref[...] = total

    def body(k, carry):
        for j in range(2):
            g = k * 2 + j
            value = jnp.zeros((8, LANES), jnp.float32)
            for c in range(3):
                base = c * modes * tiles + g * 8 * tiles
                for r in range(slots):
                    row = jnp.broadcast_to(nodal_ref[c * 16 + r : c * 16 + r + 1, :], (8, LANES))
                    if r < tiles:
                        rows = buf[pl.ds(base + r, 8, stride=tiles), :]
                    else:
                        rows = sides[r - tiles][pl.ds(pl.multiple_of(c * modes + g * 8, 8), 8), :]
                    value = value + rows * row
            acc_ref[pl.ds(pl.multiple_of(g * 8, 8), 8), :] = value
        return carry

    lax.fori_loop(0, modes // 16, body, 0)
    sums = jnp.sum(jnp.transpose(acc_ref[...]), axis=0, keepdims=True)
    out_ref[...] = jnp.broadcast_to(sums, out_ref.shape)


def final_kernel(modes, tiles, chunks, parts_ref, basis_ref, coords_ref, velocity_ref, external_ref,
                 coords_out, velocity_out, reduced_out, displaced_out, buf, sems, cols):
    copies = load_chunks(basis_ref, buf, sems, chunks)
    coords, velocity, reduced = newest(False, parts_ref, coords_ref, velocity_ref, external_ref)
    coords_out[...] = coords
    velocity_out[...] = velocity
    reduced_out[...] = reduced
    cols[...] = column(coords)
    per = chunks // 3
    for c in range(3):
        for i in range(per):
            copies[c * per + i].wait()
        for r, row in enumerate(contract(buf, cols, modes, tiles, c)):
            displaced_out[c * tiles + r : c * tiles + r + 1, :] = row


VMEM = pl.BlockSpec(memory_space=pltpu.VMEM)
ANY = pl.BlockSpec(memory_space=pl.ANY)


def step(first, parts, basis, sides, links, modulus, weight, stiffness, coords, velocity, external, devices):
    modes = coords.shape[1]
    tiles = basis.shape[0] // (3 * modes)
    chunks = 6
    elements = links.shape[1]
    slots = tiles + 4
    vector = jax.ShapeDtypeStruct((1, modes), jnp.float32)
    outs = [jax.ShapeDtypeStruct((devices, modes), jnp.float32)]
    args = [basis, *sides, links, modulus, weight, stiffness, coords, velocity, external]
    specs = [ANY] + [VMEM] * (len(args) - 1)
    if not first:
        args = [parts] + args
        specs = [VMEM] + specs
        outs += [vector, vector]
    return pl.pallas_call(
        functools.partial(step_kernel, first, modes, tiles, chunks),
        out_shape=tuple(outs),
        in_specs=specs,
        out_specs=(VMEM,) * len(outs),
        scratch_shapes=[
            pltpu.VMEM(basis.shape, jnp.float32),
            pltpu.SemaphoreType.DMA((chunks,)),
            pltpu.VMEM((modes, LANES), jnp.float32),
            pltpu.VMEM((-(-3 * slots // 8) * 8, LANES), jnp.float32),
            pltpu.VMEM((24, elements), jnp.float32),
            pltpu.VMEM((SPLITS * 48, 8 * elements), jnp.bfloat16),
            pltpu.VMEM((LANES, 8 * elements), jnp.bfloat16),
            pltpu.VMEM((48, LANES), jnp.float32),
            pltpu.VMEM((modes, LANES), jnp.float32),
        ],
        compiler_params=pltpu.CompilerParams(vmem_limit_bytes=32 * 2**20),
        name="first_step" if first else "next_step",
    )(*args)


def finish(parts, basis, coords, velocity, external):
    modes = coords.shape[1]
    tiles = basis.shape[0] // (3 * modes)
    chunks = 6
    vector = jax.ShapeDtypeStruct((1, modes), jnp.float32)
    return pl.pallas_call(
        functools.partial(final_kernel, modes, tiles, chunks),
        out_shape=(vector, vector, vector, jax.ShapeDtypeStruct((3 * tiles, LANES), jnp.float32)),
        in_specs=[VMEM, ANY, VMEM, VMEM, VMEM],
        out_specs=(VMEM,) * 4,
        scratch_shapes=[
            pltpu.VMEM(basis.shape, jnp.float32),
            pltpu.SemaphoreType.DMA((chunks,)),
            pltpu.VMEM((modes, LANES), jnp.float32),
        ],
        compiler_params=pltpu.CompilerParams(vmem_limit_bytes=16 * 2**20),
        name="finish",
    )(parts, basis, coords, velocity, external)


def shards(basis, connectivity, send_nodes, modulus, ecsw_weight, stiffness, coords, velocity, external):
    modes = coords.shape[0]
    nodes = basis.shape[3]
    flat = basis.reshape(3 * modes * nodes // LANES, LANES)
    links = connectivity[:, 0, :]
    senders = send_nodes[:, 0, :]
    coords, velocity, external = (x[None, :] for x in (coords, velocity, external))

    below_y, above_y = shared_rows(flat, senders[2:4], modes)
    n_y = lax.axis_size("gy")
    up_y = [(i, i + 1) for i in range(n_y - 1)]
    down_y = [(j, i) for i, j in up_y]
    r2 = lax.ppermute(above_y, "gy", up_y)
    r3 = lax.ppermute(below_y, "gy", down_y)
    below_x, above_x = shared_rows(flat, senders[0:2], modes)
    n_x = lax.axis_size("gx")
    up_x = [(i, i + 1) for i in range(n_x - 1)]
    down_x = [(j, i) for i, j in up_x]
    r0 = lax.ppermute(above_x, "gx", up_x)
    r1 = lax.ppermute(below_x, "gx", down_x)
    sides = (r0, r1, r2, r3)

    devices = n_x * n_y
    both = ("gx", "gy")
    (parts,) = step(True, None, flat, sides, links, modulus, ecsw_weight, stiffness, coords, velocity, external, devices)
    for _ in range(STEPS - 1):
        parts = lax.all_to_all(parts, both, 0, 0, tiled=True)
        parts, coords, velocity = step(
            False, parts, flat, sides, links, modulus, ecsw_weight, stiffness, coords, velocity, external, devices
        )
    parts = lax.all_to_all(parts, both, 0, 0, tiled=True)
    coords, velocity, reduced, displaced = finish(parts, flat, coords, velocity, external)
    return coords[0], velocity[0], reduced[0], displaced.reshape(3, 1, nodes)


def solution(mesh):
    return jax.shard_map(
        shards,
        mesh=mesh,
        in_specs=(
            P(None, None, "gx", "gy"),
            P(None, "gx", "gy"),
            P(None, "gx", "gy"),
            P("gx", "gy"),
            P("gx", "gy"),
            P(),
            P(),
            P(),
            P(),
        ),
        out_specs=(P(), P(), P(), P(None, "gx", "gy")),
        check_vma=False,
    )
```

time: 330 us -> 105 us (0.32)
  other arithmetic: 103 us -> 0 us
  local copies, waits for them, and re-layouts: 73.5 us -> 4.75 us
  matrix products: 33.3 us -> 0 us
  Pallas kernels: 0 us -> 33.1 us
  starting transfers between devices: 43.3 us -> 10.9 us
  blocking collectives: 64.3 us -> 39.8 us
  waiting for transfers between devices: 8.03 us -> 14.9 us
    scatter-add x10 -> x0, other arithmetic: 102 us -> none  [the longest x2 89.1 us: element_forces(): jnp.zeros_like(moved).at[:, links].add(forces.reshape(3, 8, links.shape[1]))]
    gather x12 -> x0, local copies, waits for them, and re-layouts: 66.2 us -> none  [the longest x4 61.1 us: element_forces(): corner = moved[:, links]]
    psum x8 -> x0, blocking collectives: 64.3 us -> none  [one_axis_at_a_time(): x = lax.psum(x, axis)]
    all_to_all x0 -> x2, blocking collectives: none -> 39.8 us  [shards(): parts = lax.all_to_all(parts, both, 0, 0, tiled=True)]
    dot_general x7 -> x0, matrix products: 33.3 us -> none  [the longest x2 15.5 us: shards(): jnp.einsum('ckn,cn->k', owned_rows, owned_force, precision=highest)]
    pallas_call x0 -> x5, Pallas kernels: none -> 33.1 us  [the longest x2 15.1 us: shared_rows(): pl.pallas_call(functools.partial(shared_rows_kernel, modes, tiles, chunks...]
    ppermute x16 -> x4, starting transfers between devices: 43.3 us -> 10.9 us  [the longest x1 4.58 us: shards(): r0 = lax.ppermute(above_x, 'gx', up_x)]
    ppermute x16 -> x4, waiting for transfers between devices: 8.03 us -> 14.9 us  [the longest x1 10.8 us: shards(): r2 = lax.ppermute(above_y, 'gy', up_y)]
  transfers between devices with their start and end apart: 16 -> 4, of which waited for: 3 -> 2; matrix products, arithmetic and copies ran while one was open for 4% -> 0% of each run, Pallas kernels for 0% -> 7%
where the time goes in v1:
time: 105 us; the launch traced here: 104 us
  blocking collectives  39.8 us (38%)
  Pallas kernels  33.1 us (32%)
  waiting for transfers between devices  14.9 us (14%)
  starting transfers between devices  10.9 us (10%)
  local copies, waits for them, and re-layouts  4.75 us (5%)
    all_to_all x2, blocking collectives, shards(): parts = lax.all_to_all(parts, both, 0, 0, tiled=True)  39.8 us
    pallas_call x2, Pallas kernels, shared_rows(): pl.pallas_call(functools.partial(shared_rows_kernel, modes, tiles, chunks...  15.1 us
    pallas_call x2, Pallas kernels, step(): pl.pallas_call(functools.partial(step_kernel, first, modes, tiles, chunks...  14.5 us
    ppermute x1, waiting for transfers between devices, shards(): r2 = lax.ppermute(above_y, 'gy', up_y)  10.8 us
    ppermute x1, starting transfers between devices, shards(): r0 = lax.ppermute(above_x, 'gx', up_x)  4.58 us
    ppermute x1, waiting for transfers between devices, shards(): r3 = lax.ppermute(below_y, 'gy', down_y)  4.14 us
    pallas_call x1, Pallas kernels, finish(): pl.pallas_call(functools.partial(final_kernel, modes, tiles, chunks), out...  3.51 us
    ppermute x1, starting transfers between devices, shards(): r2 = lax.ppermute(above_y, 'gy', up_y)  3.15 us
  transfers between devices with their start and end apart: 4, of which 2 were waited for; matrix products, arithmetic and copies ran while one was open for 0% of the time, Pallas kernels for 7%

profile of v1, /device:TPU:1, one launch (start us, length us, event | category | flops | bytes accessed | tf_op | source)
XLA Modules:
  0.0 104.4 jit_solution(12760264026423592291)
XLA Ops:
  0.6 0.8 slice_bitcast_fusion
  1.4 0.0 copy-start
  1.4 2.7 %copy-done = f32[3,400,1,1280]{3,2,1,0:T(1,128)S(1)} copy-done((f32[3,400,1,1280]{3,2,1,0:T(1,128)S(1)}, f32[3,400,1,1280]{3,2,1,0:T(1,128)}, u32[]{:S(2)}) %copy-start) | copy-done | bytes 6144024
  4.1 0.0 copy-start.8
  4.1 0.0 copy-start.1
  4.1 0.0 copy-start.2
  4.1 0.0 copy-start.3
  4.1 0.0 copy-start.4
  4.2 0.0 copy-start.5
  4.2 0.0 copy-start.6
  4.2 0.0 copy-start.7
  4.2 7.6 %shared_rows.2 = (f32[1200,128]{1,0:T(8,128)S(1)}, f32[1200,128]{1,0:T(8,128)S(1)}) custom-call(f32[12000,128]{1,0:T(8,128)S(1)} %bitcast.25, s32[2,128]{1,0:T(2,128)S(1)} %get-tuple-element.43.send_ref), custom_call_target="tpu_custom_call" | custom-call | tf_op jit(solution)/shard_map/shared_rows/pallas_call | solution.py:63
  11.8 4.6 %collective-permute-start = (f32[1200,128]{1,0:T(8,128)S(1)}, f32[1200,128]{1,0:T(8,128)S(1)}, u32[]{:S(2)}, u32[]{:S(2)}) collective-permute-start(f32[1200,128]{1,0:T(8,128)S(1)} %get-tuple-element.15), channel_id=1, source_target_pairs={{0,16},{16,32},{32,48},{48,64},{64,80},{80,96},{96,112},{1,17},{17... | collective-permute-start | bytes 1843208 | tf_op jit(solution)/shard_map/ppermute | solution.py:313
  16.4 1.9 %collective-permute-start.1 = (f32[1200,128]{1,0:T(8,128)S(1)}, f32[1200,128]{1,0:T(8,128)S(1)}, u32[]{:S(2)}, u32[]{:S(2)}) collective-permute-start(f32[1200,128]{1,0:T(8,128)S(1)} %get-tuple-element.16), channel_id=1, source_target_pairs={{16,0},{32,16},{48,32},{64,48},{80,64},{96,80},{112,96},{17,1},{33... | collective-permute-start | bytes 1843208 | tf_op jit(solution)/shard_map/ppermute | solution.py:314
  18.3 7.6 %shared_rows.3 = (f32[1200,128]{1,0:T(8,128)S(1)}, f32[1200,128]{1,0:T(8,128)S(1)}) custom-call(f32[12000,128]{1,0:T(8,128)S(1)} %bitcast.26, s32[2,128]{1,0:T(2,128)S(1)} %get-tuple-element.42.send_ref), custom_call_target="tpu_custom_call" | custom-call | tf_op jit(solution)/shard_map/shared_rows/pallas_call | solution.py:63
  25.9 3.2 %collective-permute-start.2 = (f32[1200,128]{1,0:T(8,128)S(1)}, f32[1200,128]{1,0:T(8,128)S(1)}, u32[]{:S(2)}, u32[]{:S(2)}) collective-permute-start(f32[1200,128]{1,0:T(8,128)S(1)} %get-tuple-element.17), channel_id=1, source_target_pairs={{0,1},{1,2},{2,3},{3,4},{4,5},{5,6},{6,7},{7,8},{8,9},{9,10},{10,1... | collective-permute-start | bytes 1843208 | tf_op jit(solution)/shard_map/ppermute | solution.py:307
  29.0 1.3 %collective-permute-start.3 = (f32[1200,128]{1,0:T(8,128)S(1)}, f32[1200,128]{1,0:T(8,128)S(1)}, u32[]{:S(2)}, u32[]{:S(2)}) collective-permute-start(f32[1200,128]{1,0:T(8,128)S(1)} %get-tuple-element.18), channel_id=1, source_target_pairs={{1,0},{2,1},{3,2},{4,3},{5,4},{6,5},{7,6},{8,7},{9,8},{10,9},{11,1... | collective-permute-start | bytes 1843208 | tf_op jit(solution)/shard_map/ppermute | solution.py:308
  30.3 0.0 copy-done.8
  30.3 0.0 collective-permute-done.refs_1_.refs_2_
  30.4 0.0 collective-permute-done.1.refs_2_.refs_3_
  30.4 10.8 %collective-permute-done.2.refs_3_.refs_4_ = f32[1200,128]{1,0:T(8,128)S(1)} collective-permute-done((f32[1200,128]{1,0:T(8,128)S(1)}, f32[1200,128]{1,0:T(8,128)S(1)}, u32[]{:S(2)}, u32[]{:S(2)}) %collective-permute-start.2) | collective-permute-done | bytes 614432 | tf_op jit(solution)/shard_map/ppermute | solution.py:307
  41.2 4.1 %collective-permute-done.3.refs_4_.refs_5_ = f32[1200,128]{1,0:T(8,128)S(1)} collective-permute-done((f32[1200,128]{1,0:T(8,128)S(1)}, f32[1200,128]{1,0:T(8,128)S(1)}, u32[]{:S(2)}, u32[]{:S(2)}) %collective-permute-start.3) | collective-permute-done | bytes 614432 | tf_op jit(solution)/shard_map/ppermute | solution.py:308
  45.3 0.0 copy-done.1
  45.3 0.0 copy-done.2
  45.3 0.0 copy-done.3
  45.3 0.0 copy-done.4
  45.3 0.0 copy-done.5
  45.3 0.0 copy-done.6
  45.3 0.0 copy-done.7
  45.3 7.1 %first_step.1 = f32[128,400]{1,0:T(8,128)S(1)} custom-call(f32[12000,128]{1,0:T(8,128)S(1)} %bitcast.27, f32[1200,128]{1,0:T(8,128)S(1)} %collective-permute-done.refs_1_.refs_2_, f32[1200,128]{1,0:T(8,128)S(1)} %collective-permute-done.1.refs_2_.refs_3_, f32[1200,128]{1,0:T(8,128)S(1)} %collective-permute-done.2.refs_3_.refs_4_, ...), custom_call_target="tpu_custom_call" | custom-call | tf_op jit(solution)/shard_map/first_step/pallas_call | solution.py:254
  52.5 0.3 copy.26
  52.8 24.5 %all_to_all.22 = f32[128,1,400]{2,1,0:T(1,128)S(1)} all-to-all(f32[128,1,400]{2,1,0:T(1,128)S(1)} %copy.26), channel_id=1, replica_groups=mesh['gx'=8,'gy'=16] {'gx','gy'}, dimensions={0} | all-to-all | bytes 409600 | tf_op jit(solution)/shard_map/all_to_all | solution.py:321
  77.3 7.3 %next_step.1 = (f32[128,400]{1,0:T(8,128)S(1)}, f32[1,400]{1,0:T(1,128)S(1)}, f32[1,400]{1,0:T(1,128)S(1)}) custom-call(f32[128,400]{1,0:T(8,128)S(1)} %bitcast.30, f32[12000,128]{1,0:T(8,128)S(1)} %bitcast.28, f32[1200,128]{1,0:T(8,128)S(1)} %collective-permute-done.refs_1_.refs_2_, f32[1200,128]{1,0:T(8,128)S(1)} %collective-permute-done.1.refs_2_.refs_3_, ...), custom_call_target="tpu_custom_call" | custom-call | tf_op jit(solution)/shard_map/next_step/pallas_call | solution.py:254
  84.7 0.3 copy.29
  85.0 15.2 %all_to_all.23 = f32[128,1,400]{2,1,0:T(1,128)S(1)} all-to-all(f32[128,1,400]{2,1,0:T(1,128)S(1)} %copy.29), channel_id=1, replica_groups=mesh['gx'=8,'gy'=16] {'gx','gy'}, dimensions={0} | all-to-all | bytes 409600 | tf_op jit(solution)/shard_map/all_to_all | solution.py:325
  100.2 3.5 %finish.1 = (f32[1,400]{1,0:T(1,128)}, f32[1,400]{1,0:T(1,128)}, f32[1,400]{1,0:T(1,128)}, f32[30,128]{1,0:T(8,128)S(1)}) custom-call(f32[128,400]{1,0:T(8,128)S(1)} %bitcast.31, f32[12000,128]{1,0:T(8,128)S(1)} %bitcast.29, f32[1,400]{1,0:T(1,128)S(1)} %get-tuple-element.20.coords_ref, f32[1,400]{1,0:T(1,128)S(1)} %get-tuple-element.21.velocity_ref, ...), custom_call_target="tpu_custom_call" | custom-call | tf_op jit(solution)/shard_map/finish/pallas_call | solution.py:280
  103.7 0.6 reshape.22
  (3 shorter events, 0.0 us)
Async XLA Ops:
  1.4 2.7 %copy-start = (f32[3,400,1,1280]{3,2,1,0:T(1,128)S(1)}, f32[3,400,1,1280]{3,2,1,0:T(1,128)}, u32[]{:S(2)}) copy-start(f32[3,400,1,1280]{3,2,1,0:T(1,128)} %param.9) | copy-start | bytes 18432004
  4.1 26.2 %copy-start.8 = (s32[8,1,1024]{2,1,0:T(1,128)S(1)}, s32[8,1,1024]{2,1,0:T(1,128)}, u32[]{:S(2)}) copy-start(s32[8,1,1024]{2,1,0:T(1,128)} %param.10) | copy-start | bytes 98308
  4.1 41.2 %copy-start.1 = (f32[3,400,1,1280]{3,2,1,0:T(1,128)S(1)}, f32[3,400,1,1280]{3,2,1,0:T(1,128)}, u32[]{:S(2)}) copy-start(f32[3,400,1,1280]{3,2,1,0:T(1,128)} %param.9) | copy-start | bytes 18432004
  4.1 41.2 %copy-start.2 = (f32[24,24]{1,0:T(8,128)S(1)}, f32[24,24]{1,0:T(8,128)}, u32[]{:S(2)}) copy-start(f32[24,24]{1,0:T(8,128)} %refs_9_.1) | copy-start | bytes 6916
  4.1 41.2 %copy-start.3 = (f32[400]{0:T(512)S(1)}, f32[400]{0:T(512)}, u32[]{:S(2)}) copy-start(f32[400]{0:T(512)} %param.17) | copy-start | bytes 4804
  4.1 41.2 %copy-start.4 = (f32[1,1024]{1,0:T(1,128)S(1)}, f32[1,1024]{1,0:T(1,128)}, u32[]{:S(2)}) copy-start(f32[1,1024]{1,0:T(1,128)} %refs_7_.3) | copy-start | bytes 12292
  4.2 41.2 %copy-start.5 = (f32[1,1024]{1,0:T(1,128)S(1)}, f32[1,1024]{1,0:T(1,128)}, u32[]{:S(2)}) copy-start(f32[1,1024]{1,0:T(1,128)} %refs_8_.3) | copy-start | bytes 12292
  4.2 41.2 %copy-start.6 = (f32[400]{0:T(512)S(1)}, f32[400]{0:T(512)}, u32[]{:S(2)}) copy-start(f32[400]{0:T(512)} %param.15) | copy-start | bytes 4804
  4.2 41.2 %copy-start.7 = (f32[400]{0:T(512)S(1)}, f32[400]{0:T(512)}, u32[]{:S(2)}) copy-start(f32[400]{0:T(512)} %param.16) | copy-start | bytes 4804
  11.8 18.6 %collective-permute-start = (f32[1200,128]{1,0:T(8,128)S(1)}, f32[1200,128]{1,0:T(8,128)S(1)}, u32[]{:S(2)}, u32[]{:S(2)}) collective-permute-start(f32[1200,128]{1,0:T(8,128)S(1)} %get-tuple-element.15), channel_id=1, source_target_pairs={{0,16},{16,32},{32,48},{48,64},{64,80},{80,96},{96,112},{1,17},{17... | collective-permute-start | bytes 1843208 | tf_op jit(solution)/shard_map/ppermute | solution.py:313
  16.4 14.0 %collective-permute-start.1 = (f32[1200,128]{1,0:T(8,128)S(1)}, f32[1200,128]{1,0:T(8,128)S(1)}, u32[]{:S(2)}, u32[]{:S(2)}) collective-permute-start(f32[1200,128]{1,0:T(8,128)S(1)} %get-tuple-element.16), channel_id=1, source_target_pairs={{16,0},{32,16},{48,32},{64,48},{80,64},{96,80},{112,96},{17,1},{33... | collective-permute-start | bytes 1843208 | tf_op jit(solution)/shard_map/ppermute | solution.py:314
  25.9 15.3 %collective-permute-start.2 = (f32[1200,128]{1,0:T(8,128)S(1)}, f32[1200,128]{1,0:T(8,128)S(1)}, u32[]{:S(2)}, u32[]{:S(2)}) collective-permute-start(f32[1200,128]{1,0:T(8,128)S(1)} %get-tuple-element.17), channel_id=1, source_target_pairs={{0,1},{1,2},{2,3},{3,4},{4,5},{5,6},{6,7},{7,8},{8,9},{9,10},{10,1... | collective-permute-start | bytes 1843208 | tf_op jit(solution)/shard_map/ppermute | solution.py:307
  29.0 16.3 %collective-permute-start.3 = (f32[1200,128]{1,0:T(8,128)S(1)}, f32[1200,128]{1,0:T(8,128)S(1)}, u32[]{:S(2)}, u32[]{:S(2)}) collective-permute-start(f32[1200,128]{1,0:T(8,128)S(1)} %get-tuple-element.18), channel_id=1, source_target_pairs={{1,0},{2,1},{3,2},{4,3},{5,4},{6,5},{7,6},{8,7},{9,8},{10,9},{11,1... | collective-permute-start | bytes 1843208 | tf_op jit(solution)/shard_map/ppermute | solution.py:308

commit v2 on v0

v2 whole, which is shorter than its diff:
```python
import functools

import jax
import jax.numpy as jnp
from jax import lax
from jax.experimental import pallas as pl
from jax.experimental.pallas import tpu as pltpu
from jax.sharding import PartitionSpec as P

STEPS = 2
DT = 0.05
LANES = 128
SPLITS = 3
MIB = 2**20

VMEM = pl.BlockSpec(memory_space=pltpu.VMEM)
HBM = pl.BlockSpec(memory_space=pltpu.HBM)


def lane_pick(rows, lanes):
    return jnp.take_along_axis(rows, lanes, axis=1, mode="promise_in_bounds")


def eight(start):
    return pl.ds(pl.multiple_of(start, 8), 8)


def picks_of(send_ref, sides):
    picks = []
    for side in sides:
        nodes = jnp.broadcast_to(send_ref[side], (8, LANES))
        picks.append((nodes & (LANES - 1), nodes >> 7))
    return picks


def pick_rows(tiles, picks):
    sums = [jnp.zeros((8, LANES), jnp.float32) for _ in picks]
    for t, rows in enumerate(tiles):
        for side, (lanes, tile) in enumerate(picks):
            sums[side] = jnp.where(tile == t, lane_pick(rows, lanes), sums[side])
    return sums


def load_kernel(modes, tiles, chunks, basis_ref, send_ref, dense_ref, below_ref, above_ref, buf, sems):
    size = buf.shape[0] // chunks
    copies = [
        pltpu.make_async_copy(
            basis_ref.at[pl.ds(i * size, size)], buf.at[pl.ds(i * size, size)], sems.at[i]
        )
        for i in range(chunks)
    ]
    for copy in copies:
        copy.start()
    picks = picks_of(send_ref, (2, 3))
    groups = size // (8 * tiles)
    per = chunks // 3
    for i in range(chunks):
        comp = i // per
        copies[i].wait()

        def body(g, carry, i=i, comp=comp):
            mode = (g + (i % per) * groups) * 8
            row = (g + i * groups) * (8 * tiles)
            read = []
            for t in range(tiles):
                rows = buf[pl.ds(row + t, 8, stride=tiles), :]
                dense_ref[eight((comp * tiles + t) * modes + mode), :] = rows
                read.append(rows)
            for ref, value in zip((below_ref, above_ref), pick_rows(read, picks)):
                ref[eight(comp * modes + mode), :] = value
            return carry

        lax.fori_loop(0, groups, body, 0, unroll=25)


def load(basis, send, modes):
    rows = basis.shape[0]
    tiles = rows // (3 * modes)
    chunks = 6
    shared = jax.ShapeDtypeStruct((3 * modes, LANES), jnp.float32)
    return pl.pallas_call(
        functools.partial(load_kernel, modes, tiles, chunks),
        out_shape=(jax.ShapeDtypeStruct(basis.shape, jnp.float32), shared, shared),
        in_specs=[HBM, VMEM],
        out_specs=(VMEM,) * 3,
        scratch_shapes=[
            pltpu.VMEM((rows, LANES), jnp.float32),
            pltpu.SemaphoreType.DMA((chunks,)),
        ],
        compiler_params=pltpu.CompilerParams(vmem_limit_bytes=24 * MIB),
        name="load",
    )(basis, send)


def share_kernel(modes, tiles, dense_ref, send_ref, below_ref, above_ref):
    picks = picks_of(send_ref, (0, 1))

    for c in range(3):

        def body(g, carry, c=c):
            read = [dense_ref[eight((c * tiles + t) * modes + g * 8), :] for t in range(tiles)]
            for ref, value in zip((below_ref, above_ref), pick_rows(read, picks)):
                ref[eight(c * modes + g * 8), :] = value
            return carry

        lax.fori_loop(0, modes // 8, body, 0, unroll=25)


def share(dense, send, modes):
    tiles = dense.shape[0] // (3 * modes)
    shared = jax.ShapeDtypeStruct((3 * modes, LANES), jnp.float32)
    return pl.pallas_call(
        functools.partial(share_kernel, modes, tiles),
        out_shape=(shared, shared),
        in_specs=[VMEM, VMEM],
        out_specs=(VMEM,) * 2,
        compiler_params=pltpu.CompilerParams(vmem_limit_bytes=16 * MIB),
        name="share",
    )(dense, send)


def column(row):
    return jnp.transpose(jnp.broadcast_to(row, (LANES, row.shape[1])))


def contract(places, cols, modes):
    def body(k, sums):
        scale = cols[eight(k * 8), :]
        return tuple(s + ref[eight(at + k * 8), :] * scale for s, (ref, at) in zip(sums, places))

    zero = jnp.zeros((8, LANES), jnp.float32)
    sums = lax.fori_loop(0, modes // 8, body, (zero,) * len(places), unroll=2)
    return [jnp.sum(s, axis=0, keepdims=True) for s in sums]


def owned_places(dense_ref, modes, tiles):
    return [(dense_ref, (c * tiles + t) * modes) for c in range(3) for t in range(tiles)]


def shared_places(sides, modes):
    return [(side, c * modes) for c in range(3) for side in sides]


def prepare_kernel(modes, tiles, dense_ref, links_ref, coords_ref, owned_ref, low_ref, high_ref, cols):
    cols[...] = column(coords_ref[...])
    for i, row in enumerate(contract(owned_places(dense_ref, modes, tiles), cols, modes)):
        owned_ref[i : i + 1, :] = row
    elements = links_ref.shape[1]
    for b in range(elements // LANES):
        for a in range(8):
            links = links_ref[a : a + 1, b * LANES : (b + 1) * LANES]
            at = slice(a * elements + b * LANES, a * elements + (b + 1) * LANES)
            for ref, bits, size in ((low_ref, links & (LANES - 1), LANES), (high_ref, links >> 7, 16)):
                count = lax.broadcasted_iota(jnp.int32, (size, LANES), 0)
                hot = jnp.broadcast_to(bits, (size, LANES)) == count
                ref[:, at] = jnp.where(hot, 1.0, 0.0).astype(jnp.bfloat16)


def prepare(dense, links, coords):
    modes = coords.shape[1]
    tiles = dense.shape[0] // (3 * modes)
    entries = 8 * links.shape[1]
    return pl.pallas_call(
        functools.partial(prepare_kernel, modes, tiles),
        out_shape=(
            jax.ShapeDtypeStruct((-(-3 * tiles // 8) * 8, LANES), jnp.float32),
            jax.ShapeDtypeStruct((LANES, entries), jnp.bfloat16),
            jax.ShapeDtypeStruct((16, entries), jnp.bfloat16),
        ),
        in_specs=[VMEM] * 3,
        out_specs=(VMEM,) * 3,
        scratch_shapes=[pltpu.VMEM((modes, LANES), jnp.float32)],
        compiler_params=pltpu.CompilerParams(vmem_limit_bytes=16 * MIB),
        name="prepare",
    )(dense, links, coords)


def advance(parts_ref, coords_ref, velocity_ref, external_ref):
    sums = jnp.sum(parts_ref[...].reshape(-1, 8, LANES), axis=0)
    pair = sums[0:4] + sums[4:8]
    modes = coords_ref.shape[1]
    reduced = jnp.concatenate([pair[r : r + 1] for r in range(4)], axis=1)[:, :modes]
    velocity = velocity_ref[...] + DT * (external_ref[...] - reduced)
    coords = coords_ref[...] + DT * velocity
    return coords, velocity, reduced


def step_kernel(first, modes, tiles, *refs):
    if first:
        (owned_ref, dense_ref, r0, r1, r2, r3, links_ref, low_ref, high_ref, modulus_ref, weight_ref, stiff_ref,
         coords_ref, out_ref, cols, table, corner, pieces, spread) = refs
        coords = coords_ref[...]
    else:
        (parts_ref, dense_ref, r0, r1, r2, r3, links_ref, low_ref, high_ref, modulus_ref, weight_ref, stiff_ref,
         coords_ref, velocity_ref, external_ref, out_ref, coords_out, velocity_out,
         cols, table, corner, pieces, spread) = refs
        coords, velocity, _ = advance(parts_ref, coords_ref, velocity_ref, external_ref)
        coords_out[...] = coords
        velocity_out[...] = velocity
    sides = (r0, r1, r2, r3)
    slots = tiles + 4
    elements = links_ref.shape[1]
    blocks = elements // LANES

    cols[...] = column(coords)
    if first:
        owned = [owned_ref[i : i + 1, :] for i in range(3 * tiles)]
        shared = contract(shared_places(sides, modes), cols, modes)
    else:
        rows = contract(
            owned_places(dense_ref, modes, tiles) + shared_places(sides, modes), cols, modes
        )
        owned, shared = rows[: 3 * tiles], rows[3 * tiles :]
    for c in range(3):
        rows = owned[c * tiles : (c + 1) * tiles] + shared[c * 4 : (c + 1) * 4]
        for r, row in enumerate(rows):
            table[c * slots + r : c * slots + r + 1, :] = row

    for b in range(blocks):
        links = links_ref[:, b * LANES : (b + 1) * LANES]
        lanes, tile = links & (LANES - 1), links >> 7
        for c in range(3):
            value = jnp.zeros((8, LANES), jnp.float32)
            for r in range(slots):
                row = jnp.broadcast_to(table[c * slots + r : c * slots + r + 1, :], (8, LANES))
                value = jnp.where(tile == r, lane_pick(row, lanes), value)
            corner[c * 8 : (c + 1) * 8, b * LANES : (b + 1) * LANES] = value

    strain = jnp.dot(
        stiff_ref[...], corner[...],
        precision=lax.Precision.HIGHEST, preferred_element_type=jnp.float32,
    )
    factor = modulus_ref[...] * weight_ref[...]
    rest = factor * (strain + strain * strain * strain * (1.0 / 3.0))
    for s in range(SPLITS):
        piece = rest.astype(jnp.bfloat16).astype(jnp.float32)
        pieces[s * 24 : (s + 1) * 24, :] = piece
        rest = rest - piece

    for b in range(blocks):
        part = slice(b * LANES, (b + 1) * LANES)
        for a in range(8):
            at = slice(a * elements + b * LANES, a * elements + (b + 1) * LANES)
            hot = high_ref[:, at]
            for g in range(SPLITS * 3):
                row = pieces[g * 8 + a : g * 8 + a + 1, part]
                value = jnp.broadcast_to(row, (16, LANES)).astype(jnp.bfloat16)
                spread[g * 16 : (g + 1) * 16, at] = hot * value
    nodal = lax.dot_general(
        spread[...], low_ref[...], (((1,), (1,)), ((), ())), preferred_element_type=jnp.float32
    )
    total = nodal[0:48]
    for s in range(1, SPLITS):
        total = total + nodal[s * 48 : (s + 1) * 48]

    places = []
    for c in range(3):
        for r in range(slots):
            row = jnp.broadcast_to(total[c * 16 + r : c * 16 + r + 1], (8, LANES))
            if r < tiles:
                places.append((dense_ref, (c * tiles + r) * modes, row))
            else:
                places.append((sides[r - tiles], c * modes, row))

    def body(k, carry):
        sums = [jnp.zeros((8, LANES), jnp.float32) for _ in range(3)]
        for i, (ref, at, row) in enumerate(places):
            sums[i % 3] = sums[i % 3] + ref[eight(at + k * 8), :] * row
        cols[eight(k * 8), :] = sums[0] + sums[1] + sums[2]
        return carry

    lax.fori_loop(0, modes // 8, body, 0, unroll=2)
    sums = jnp.sum(jnp.transpose(cols[...]), axis=0, keepdims=True)
    sums = jnp.concatenate([sums, jnp.zeros((1, 4 * LANES - modes), jnp.float32)], axis=1)
    pair = [sums[:, r * LANES : (r + 1) * LANES] for r in range(4)]
    pair = jnp.concatenate(pair + pair, axis=0)
    out_ref[...] = jnp.broadcast_to(pair[None], (out_ref.shape[0] // 8, 8, LANES)).reshape(out_ref.shape)


def step(first, parts, dense, sides, links, low, high, modulus, weight, stiffness, vectors, devices):
    modes = vectors[0].shape[1]
    tiles = dense.shape[0] // (3 * modes)
    elements = links.shape[1]
    slots = tiles + 4
    vector = jax.ShapeDtypeStruct((1, modes), jnp.float32)
    outs = [jax.ShapeDtypeStruct((devices * 4, LANES), jnp.float32)]
    args = [parts, dense, *sides, links, low, high, modulus, weight, stiffness]
    if first:
        args += vectors[:1]
    else:
        args += vectors
        outs += [vector, vector]
    return pl.pallas_call(
        functools.partial(step_kernel, first, modes, tiles),
        out_shape=tuple(outs),
        in_specs=[VMEM] * len(args),
        out_specs=(VMEM,) * len(outs),
        scratch_shapes=[
            pltpu.VMEM((modes, LANES), jnp.float32),
            pltpu.VMEM((-(-3 * slots // 8) * 8, LANES), jnp.float32),
            pltpu.VMEM((24, elements), jnp.float32),
            pltpu.VMEM((SPLITS * 24, elements), jnp.float32),
            pltpu.VMEM((SPLITS * 48, 8 * elements), jnp.bfloat16),
        ],
        compiler_params=pltpu.CompilerParams(vmem_limit_bytes=24 * MIB),
        name="first_step" if first else "next_step",
    )(*args)


def final_kernel(modes, tiles, parts_ref, dense_ref, coords_ref, velocity_ref, external_ref,
                 coords_out, velocity_out, reduced_out, displaced_out, cols):
    coords, velocity, reduced = advance(parts_ref, coords_ref, velocity_ref, external_ref)
    coords_out[...] = coords
    velocity_out[...] = velocity
    reduced_out[...] = reduced
    cols[...] = column(coords)
    for i, row in enumerate(contract(owned_places(dense_ref, modes, tiles), cols, modes)):
        c, t = divmod(i, tiles)
        displaced_out[c, :, t * LANES : (t + 1) * LANES] = row


def finish(parts, dense, vectors):
    modes = vectors[0].shape[1]
    tiles = dense.shape[0] // (3 * modes)
    vector = jax.ShapeDtypeStruct((1, modes), jnp.float32)
    return pl.pallas_call(
        functools.partial(final_kernel, modes, tiles),
        out_shape=(vector, vector, vector, jax.ShapeDtypeStruct((3, 1, tiles * LANES), jnp.float32)),
        in_specs=[VMEM] * 5,
        out_specs=(VMEM,) * 4,
        scratch_shapes=[pltpu.VMEM((modes, LANES), jnp.float32)],
        compiler_params=pltpu.CompilerParams(vmem_limit_bytes=16 * MIB),
        name="finish",
    )(parts, dense, *vectors)


def exchange(below, above, axis):
    count = lax.axis_size(axis)
    up = [(i, i + 1) for i in range(count - 1)]
    down = [(j, i) for i, j in up]
    return lax.ppermute(above, axis, up), lax.ppermute(below, axis, down)


def everyone(parts, devices):
    chunks = parts.reshape(devices, parts.shape[0] // devices, LANES)
    return lax.all_to_all(chunks, ("gx", "gy"), 0, 0, tiled=True).reshape(parts.shape)


def shards(basis, connectivity, send_nodes, modulus, ecsw_weight, stiffness, coords, velocity, external):
    modes = coords.shape[0]
    nodes = basis.shape[3]
    flat = basis.reshape(3 * modes * nodes // LANES, LANES)
    links = connectivity[:, 0, :]
    coords, velocity, external = (x[None, :] for x in (coords, velocity, external))
    devices = lax.axis_size("gx") * lax.axis_size("gy")

    flat = pltpu.with_memory_space_constraint(flat, pltpu.HBM)
    dense, below, above = load(flat, send_nodes, modes)
    r2, r3 = exchange(below, above, "gy")
    below, above = share(dense, send_nodes, modes)
    r0, r1 = exchange(below, above, "gx")
    owned, low, high = prepare(dense, links, coords)
    sides = (r0, r1, r2, r3)

    (parts,) = step(True, owned, dense, sides, links, low, high, modulus, ecsw_weight, stiffness, (coords,), devices)
    for _ in range(STEPS - 1):
        parts, coords, velocity = step(
            False, everyone(parts, devices), dense, sides, links, low, high, modulus, ecsw_weight, stiffness,
            (coords, velocity, external), devices,
        )
    coords, velocity, reduced, displaced = finish(everyone(parts, devices), dense, (coords, velocity, external))
    return coords[0], velocity[0], reduced[0], displaced


def solution(mesh):
    return jax.shard_map(
        shards,
        mesh=mesh,
        in_specs=(
            P(None, None, "gx", "gy"),
            P(None, "gx", "gy"),
            P(None, "gx", "gy"),
            P("gx", "gy"),
            P("gx", "gy"),
            P(),
            P(),
            P(),
            P(),
        ),
        out_specs=(P(), P(), P(), P(None, "gx", "gy")),
        check_vma=False,
    )
```

time: 330 us -> 77 us (0.23)
  other arithmetic: 103 us -> 0 us
  local copies, waits for them, and re-layouts: 73.5 us -> 0.73 us
  matrix products: 33.3 us -> 0 us
  starting transfers between devices: 43.3 us -> 11.2 us
  blocking collectives: 64.3 us -> 37.4 us
  Pallas kernels: 0 us -> 18.5 us
    scatter-add x10 -> x0, other arithmetic: 102 us -> none  [the longest x2 89.1 us: element_forces(): jnp.zeros_like(moved).at[:, links].add(forces.reshape(3, 8, links.shape[1]))]
    gather x12 -> x0, local copies, waits for them, and re-layouts: 66.2 us -> none  [the longest x4 61.1 us: element_forces(): corner = moved[:, links]]
    psum x8 -> x0, blocking collectives: 64.3 us -> none  [one_axis_at_a_time(): x = lax.psum(x, axis)]
    all_to_all x0 -> x2, blocking collectives: none -> 37.4 us  [everyone(): lax.all_to_all(chunks, ('gx', 'gy'), 0, 0, tiled=True).reshape(parts.shape)]
    dot_general x7 -> x0, matrix products: 33.3 us -> none  [the longest x2 15.5 us: shards(): jnp.einsum('ckn,cn->k', owned_rows, owned_force, precision=highest)]
    ppermute x16 -> x4, starting transfers between devices: 43.3 us -> 11.2 us  [exchange(): return (lax.ppermute(above, axis, up), lax.ppermute(below, axis, down))]
    pallas_call x0 -> x6, Pallas kernels: none -> 18.5 us  [the longest x2 7.09 us: step(): pl.pallas_call(functools.partial(step_kernel, first, modes, tiles), out_s...]
    reshape x2 -> x0, local copies, waits for them, and re-layouts: 5.3 us -> none  [element_forces(): forces.reshape(3, 8, links.shape[1])]
  transfers between devices with their start and end apart: 16 -> 4, of which waited for: 3 -> 3; matrix products, arithmetic and copies ran while one was open for 4% -> 0% of each run, Pallas kernels for 0% -> 7%
where the time goes in v2:
time: 77 us; the launch traced here: 76.7 us
  blocking collectives  37.4 us (49%)
  Pallas kernels  18.5 us (24%)
  starting transfers between devices  11.2 us (15%)
  waiting for transfers between devices  8.06 us (10%)
  between operations  0.79 us (1%)
    all_to_all x2, blocking collectives, everyone(): lax.all_to_all(chunks, ('gx', 'gy'), 0, 0, tiled=True).reshape(parts.shape)  37.4 us
    ppermute x4, starting transfers between devices, exchange(): return (lax.ppermute(above, axis, up), lax.ppermute(below, axis, down))  11.2 us
    ppermute x4, waiting for transfers between devices, exchange(): return (lax.ppermute(above, axis, up), lax.ppermute(below, axis, down))  8.06 us
    pallas_call x2, Pallas kernels, step(): pl.pallas_call(functools.partial(step_kernel, first, modes, tiles), out_s...  7.09 us
    pallas_call x1, Pallas kernels, load(): pl.pallas_call(functools.partial(load_kernel, modes, tiles, chunks), out_...  4.89 us
    pallas_call x1, Pallas kernels, share(): pl.pallas_call(functools.partial(share_kernel, modes, tiles), out_shape=(...  3.59 us
  transfers between devices with their start and end apart: 4, of which 3 were waited for; matrix products, arithmetic and copies ran while one was open for 0% of the time, Pallas kernels for 7%

profile of v2, /device:TPU:1, one launch (start us, length us, event | category | flops | bytes accessed | tf_op | source)
XLA Modules:
  0.0 76.7 jit_solution(2774614894415671640)
XLA Ops:
  0.6 0.0 copy-start.4
  0.6 0.7 copy-done.4
  1.3 0.0 copy-start.5
  1.3 0.0 copy-start.8
  1.3 0.0 copy-start.1
  1.3 4.9 %load.1 = (f32[12000,128]{1,0:T(8,128)S(1)}, f32[1200,128]{1,0:T(8,128)S(1)}, f32[1200,128]{1,0:T(8,128)S(1)}) custom-call(f32[12000,128]{1,0:T(8,128)} %bitcast.27, s32[4,1,128]{2,1,0:T(1,128)S(1)} %copy-done.4), custom_call_target="tpu_custom_call" | custom-call | tf_op jit(solution)/shard_map/load/pallas_call | solution.py:81
  6.2 4.0 %collective-permute-start.2 = (f32[1200,128]{1,0:T(8,128)S(1)}, f32[1200,128]{1,0:T(8,128)S(1)}, u32[]{:S(2)}, u32[]{:S(2)}) collective-permute-start(f32[1200,128]{1,0:T(8,128)S(1)} %get-tuple-element.23), channel_id=1, source_target_pairs={{0,1},{1,2},{2,3},{3,4},{4,5},{5,6},{6,7},{7,8},{8,9},{9,10},{10,1... | collective-permute-start | bytes 1843208 | tf_op jit(solution)/shard_map/ppermute | solution.py:341
  10.2 1.3 %collective-permute-start.3 = (f32[1200,128]{1,0:T(8,128)S(1)}, f32[1200,128]{1,0:T(8,128)S(1)}, u32[]{:S(2)}, u32[]{:S(2)}) collective-permute-start(f32[1200,128]{1,0:T(8,128)S(1)} %get-tuple-element.24), channel_id=1, source_target_pairs={{1,0},{2,1},{3,2},{4,3},{5,4},{6,5},{7,6},{8,7},{9,8},{10,9},{11,1... | collective-permute-start | bytes 1843208 | tf_op jit(solution)/shard_map/ppermute | solution.py:341
  11.5 0.0 copy-done.5
  11.5 0.0 copy-start
  11.5 0.0 copy-start.2
  11.5 0.0 copy-start.3
  11.5 3.6 %share.1 = (f32[1200,128]{1,0:T(8,128)S(1)}, f32[1200,128]{1,0:T(8,128)S(1)}) custom-call(f32[12000,128]{1,0:T(8,128)S(1)} %get-tuple-element.19.dense_ref.refs_1_, s32[4,1,128]{2,1,0:T(1,128)S(1)} %copy-done.5), custom_call_target="tpu_custom_call" | custom-call | tf_op jit(solution)/shard_map/share/pallas_call | solution.py:112
  15.1 4.0 %collective-permute-start = (f32[1200,128]{1,0:T(8,128)S(1)}, f32[1200,128]{1,0:T(8,128)S(1)}, u32[]{:S(2)}, u32[]{:S(2)}) collective-permute-start(f32[1200,128]{1,0:T(8,128)S(1)} %get-tuple-element.21), channel_id=1, source_target_pairs={{0,16},{16,32},{32,48},{48,64},{64,80},{80,96},{96,112},{1,17},{17... | collective-permute-start | bytes 1843208 | tf_op jit(solution)/shard_map/ppermute | solution.py:341
  19.2 1.9 %collective-permute-start.1 = (f32[1200,128]{1,0:T(8,128)S(1)}, f32[1200,128]{1,0:T(8,128)S(1)}, u32[]{:S(2)}, u32[]{:S(2)}) collective-permute-start(f32[1200,128]{1,0:T(8,128)S(1)} %get-tuple-element.22), channel_id=1, source_target_pairs={{16,0},{32,16},{48,32},{64,48},{80,64},{96,80},{112,96},{17,1},{33... | collective-permute-start | bytes 1843208 | tf_op jit(solution)/shard_map/ppermute | solution.py:341
  21.1 0.0 copy-done.8
  21.1 0.0 copy-done.1
  21.2 1.4 %prepare.1 = (f32[32,128]{1,0:T(8,128)S(1)}, bf16[128,8192]{1,0:T(8,128)(2,1)S(1)}, bf16[16,8192]{1,0:T(8,128)(2,1)S(1)}) custom-call(f32[12000,128]{1,0:T(8,128)S(1)} %get-tuple-element.19.dense_ref.refs_1_, s32[8,1024]{1,0:T(8,128)S(1)} %bitcast.17, f32[1,400]{1,0:T(1,128)S(1)} %bitcast.21), custom_call_target="tpu_custom_call" | custom-call | tf_op jit(solution)/shard_map/prepare/pallas_call | solution.py:163
  22.6 0.0 copy-start.6
  22.6 0.0 copy-start.7
  22.6 0.1 collective-permute-done.2.refs_4_
  22.7 3.9 %collective-permute-done.3.refs_5_ = f32[1200,128]{1,0:T(8,128)S(1)} collective-permute-done((f32[1200,128]{1,0:T(8,128)S(1)}, f32[1200,128]{1,0:T(8,128)S(1)}, u32[]{:S(2)}, u32[]{:S(2)}) %collective-permute-start.3) | collective-permute-done | bytes 614432 | tf_op jit(solution)/shard_map/ppermute | solution.py:341
  26.6 0.0 collective-permute-done.refs_2_
  26.6 4.1 %collective-permute-done.1.refs_3_ = f32[1200,128]{1,0:T(8,128)S(1)} collective-permute-done((f32[1200,128]{1,0:T(8,128)S(1)}, f32[1200,128]{1,0:T(8,128)S(1)}, u32[]{:S(2)}, u32[]{:S(2)}) %collective-permute-start.1) | collective-permute-done | bytes 614432 | tf_op jit(solution)/shard_map/ppermute | solution.py:341
  30.7 0.0 copy-done
  30.7 0.0 copy-done.2
  30.7 0.0 copy-done.3
  30.7 3.2 %first_step.1 = f32[512,128]{1,0:T(8,128)S(1)} custom-call(f32[32,128]{1,0:T(8,128)S(1)} %get-tuple-element.20.refs_0_, f32[12000,128]{1,0:T(8,128)S(1)} %get-tuple-element.19.dense_ref.refs_1_, f32[1200,128]{1,0:T(8,128)S(1)} %collective-permute-done.refs_2_, f32[1200,128]{1,0:T(8,128)S(1)} %collective-permute-done.1.refs_3_, ...), custom_call_target="tpu_custom_call" | custom-call | tf_op jit(solution)/shard_map/first_step/pallas_call | solution.py:293
  33.9 22.2 %all_to_all.10 = f32[128,4,128]{2,1,0:T(4,128)S(1)} all-to-all(f32[128,4,128]{2,1,0:T(4,128)S(1)} %bitcast.16), channel_id=1, replica_groups=mesh['gx'=8,'gy'=16] {'gx','gy'}, dimensions={0} | all-to-all | bytes 524288 | tf_op jit(solution)/shard_map/all_to_all | solution.py:346
  56.1 0.0 copy-done.6
  56.1 0.0 copy-done.7
  56.1 3.9 %next_step.1 = (f32[512,128]{1,0:T(8,128)S(1)}, f32[1,400]{1,0:T(1,128)S(1)}, f32[1,400]{1,0:T(1,128)S(1)}) custom-call(f32[512,128]{1,0:T(8,128)S(1)} %bitcast.14, f32[12000,128]{1,0:T(8,128)S(1)} %get-tuple-element.19.dense_ref.refs_1_, f32[1200,128]{1,0:T(8,128)S(1)} %collective-permute-done.refs_2_, f32[1200,128]{1,0:T(8,128)S(1)} %collective-permute-done.1.refs_3_, ...), custom_call_target="tpu_custom_call" | custom-call | tf_op jit(solution)/shard_map/next_step/pallas_call | solution.py:293
  60.0 15.2 %all_to_all.11 = f32[128,4,128]{2,1,0:T(4,128)S(1)} all-to-all(f32[128,4,128]{2,1,0:T(4,128)S(1)} %bitcast.20), channel_id=1, replica_groups=mesh['gx'=8,'gy'=16] {'gx','gy'}, dimensions={0} | all-to-all | bytes 524288 | tf_op jit(solution)/shard_map/all_to_all | solution.py:346
  75.2 1.5 %finish.1 = (f32[1,400]{1,0:T(1,128)}, f32[1,400]{1,0:T(1,128)}, f32[1,400]{1,0:T(1,128)}, f32[3,1,1280]{2,1,0:T(1,128)}) custom-call(f32[512,128]{1,0:T(8,128)S(1)} %bitcast.15, f32[12000,128]{1,0:T(8,128)S(1)} %get-tuple-element.19.dense_ref.refs_1_, f32[1,400]{1,0:T(1,128)S(1)} %get-tuple-element.28.coords_ref, ...), custom_call_target="tpu_custom_call" | custom-call | tf_op jit(solution)/shard_map/finish/pallas_call | solution.py:326
  (1 shorter events, 0.0 us)
Async XLA Ops:
  0.6 0.7 copy-start.4
  1.3 10.2 %copy-start.5 = (s32[4,1,128]{2,1,0:T(1,128)S(1)}, s32[4,1,128]{2,1,0:T(1,128)}, u32[]{:S(2)}) copy-start(s32[4,1,128]{2,1,0:T(1,128)} %send_ref.3) | copy-start | bytes 6148
  1.3 19.8 %copy-start.8 = (s32[8,1,1024]{2,1,0:T(1,128)S(1)}, s32[8,1,1024]{2,1,0:T(1,128)}, u32[]{:S(2)}) copy-start(s32[8,1,1024]{2,1,0:T(1,128)} %param.10) | copy-start | bytes 98308
  1.3 19.8 %copy-start.1 = (f32[400]{0:T(512)S(1)}, f32[400]{0:T(512)}, u32[]{:S(2)}) copy-start(f32[400]{0:T(512)} %param.15) | copy-start | bytes 4804
  6.2 16.5 %collective-permute-start.2 = (f32[1200,128]{1,0:T(8,128)S(1)}, f32[1200,128]{1,0:T(8,128)S(1)}, u32[]{:S(2)}, u32[]{:S(2)}) collective-permute-start(f32[1200,128]{1,0:T(8,128)S(1)} %get-tuple-element.23), channel_id=1, source_target_pairs={{0,1},{1,2},{2,3},{3,4},{4,5},{5,6},{6,7},{7,8},{8,9},{9,10},{10,1... | collective-permute-start | bytes 1843208 | tf_op jit(solution)/shard_map/ppermute | solution.py:341
  10.2 16.4 %collective-permute-start.3 = (f32[1200,128]{1,0:T(8,128)S(1)}, f32[1200,128]{1,0:T(8,128)S(1)}, u32[]{:S(2)}, u32[]{:S(2)}) collective-permute-start(f32[1200,128]{1,0:T(8,128)S(1)} %get-tuple-element.24), channel_id=1, source_target_pairs={{1,0},{2,1},{3,2},{4,3},{5,4},{6,5},{7,6},{8,7},{9,8},{10,9},{11,1... | collective-permute-start | bytes 1843208 | tf_op jit(solution)/shard_map/ppermute | solution.py:341
  11.5 19.2 %copy-start = (f32[24,24]{1,0:T(8,128)S(1)}, f32[24,24]{1,0:T(8,128)}, u32[]{:S(2)}) copy-start(f32[24,24]{1,0:T(8,128)} %refs_11_.3) | copy-start | bytes 6916
  11.5 19.1 %copy-start.2 = (f32[1,1024]{1,0:T(1,128)S(1)}, f32[1,1024]{1,0:T(1,128)}, u32[]{:S(2)}) copy-start(f32[1,1024]{1,0:T(1,128)} %refs_9_.3) | copy-start | bytes 12292
  11.5 19.1 %copy-start.3 = (f32[1,1024]{1,0:T(1,128)S(1)}, f32[1,1024]{1,0:T(1,128)}, u32[]{:S(2)}) copy-start(f32[1,1024]{1,0:T(1,128)} %refs_10_.3) | copy-start | bytes 12292
  15.1 11.4 %collective-permute-start = (f32[1200,128]{1,0:T(8,128)S(1)}, f32[1200,128]{1,0:T(8,128)S(1)}, u32[]{:S(2)}, u32[]{:S(2)}) collective-permute-start(f32[1200,128]{1,0:T(8,128)S(1)} %get-tuple-element.21), channel_id=1, source_target_pairs={{0,16},{16,32},{32,48},{48,64},{64,80},{80,96},{96,112},{1,17},{17... | collective-permute-start | bytes 1843208 | tf_op jit(solution)/shard_map/ppermute | solution.py:341
  19.2 11.5 %collective-permute-start.1 = (f32[1200,128]{1,0:T(8,128)S(1)}, f32[1200,128]{1,0:T(8,128)S(1)}, u32[]{:S(2)}, u32[]{:S(2)}) collective-permute-start(f32[1200,128]{1,0:T(8,128)S(1)} %get-tuple-element.22), channel_id=1, source_target_pairs={{16,0},{32,16},{48,32},{64,48},{80,64},{96,80},{112,96},{17,1},{33... | collective-permute-start | bytes 1843208 | tf_op jit(solution)/shard_map/ppermute | solution.py:341
  22.6 33.5 %copy-start.6 = (f32[400]{0:T(512)S(1)}, f32[400]{0:T(512)}, u32[]{:S(2)}) copy-start(f32[400]{0:T(512)} %param.17) | copy-start | bytes 4804
  22.6 33.5 %copy-start.7 = (f32[400]{0:T(512)S(1)}, f32[400]{0:T(512)}, u32[]{:S(2)}) copy-start(f32[400]{0:T(512)} %param.16) | copy-start | bytes 4804

commit v3 on v2

--- a/solution.py
+++ b/solution.py
@@ -11,6 +11,7 @@
 DT = 0.05
 LANES = 128
 SPLITS = 3
+CHUNKS = 6
 MIB = 2**20
 
 VMEM = pl.BlockSpec(memory_space=pltpu.VMEM)
@@ -25,23 +26,8 @@
     return pl.ds(pl.multiple_of(start, 8), 8)
 
 
-def picks_of(send_ref, sides):
-    picks = []
-    for side in sides:
-        nodes = jnp.broadcast_to(send_ref[side], (8, LANES))
-        picks.append((nodes & (LANES - 1), nodes >> 7))
-    return picks
-
-
-def pick_rows(tiles, picks):
-    sums = [jnp.zeros((8, LANES), jnp.float32) for _ in picks]
-    for t, rows in enumerate(tiles):
-        for side, (lanes, tile) in enumerate(picks):
-            sums[side] = jnp.where(tile == t, lane_pick(rows, lanes), sums[side])
-    return sums
-
-
-def load_kernel(modes, tiles, chunks, basis_ref, send_ref, dense_ref, below_ref, above_ref, buf, sems):
+def load_kernel(modes, tiles, chunks, basis_ref, send_hbm, dense_ref, *refs):
+    outs, (buf, send_ref, hot_ref, sems, send_sem) = refs[:4], refs[4:]
     size = buf.shape[0] // chunks
     copies = [
         pltpu.make_async_copy(
@@ -49,74 +35,83 @@
         )
         for i in range(chunks)
     ]
+    lists = pltpu.make_async_copy(send_hbm, send_ref, send_sem)
+    lists.start()
     for copy in copies:
         copy.start()
-    picks = picks_of(send_ref, (2, 3))
+    lists.wait()
+
+    picks = []
+    for side in range(2):
+        nodes = jnp.broadcast_to(send_ref[side], (8, LANES))
+        picks.append((nodes & (LANES - 1), nodes >> 7))
+    for t in range(tiles):
+        count = lax.broadcasted_iota(jnp.int32, (LANES, LANES), 0) + t * LANES
+        for side in range(2):
+            hot = jnp.broadcast_to(send_ref[2 + side], (LANES, LANES)) == count
+            hot_ref[t * LANES : (t + 1) * LANES, side * LANES : (side + 1) * LANES] = jnp.where(
+                hot, 1.0, 0.0
+            ).astype(jnp.bfloat16)
+
     groups = size // (8 * tiles)
     per = chunks // 3
     for i in range(chunks):
-        comp = i // per
         copies[i].wait()
-
-        def body(g, carry, i=i, comp=comp):
-            mode = (g + (i % per) * groups) * 8
-            row = (g + i * groups) * (8 * tiles)
-            read = []
-            for t in range(tiles):
-                rows = buf[pl.ds(row + t, 8, stride=tiles), :]
-                dense_ref[eight((comp * tiles + t) * modes + mode), :] = rows
-                read.append(rows)
-            for ref, value in zip((below_ref, above_ref), pick_rows(read, picks)):
-                ref[eight(comp * modes + mode), :] = value
-            return carry
-
-        lax.fori_loop(0, groups, body, 0, unroll=25)
+        comp, first = i // per, (i % per) * groups * 8
+        columns = []
+        for t in range(tiles):
+            parts = [buf[pl.ds((i * groups + g) * 8 * tiles + t, 8, stride=tiles), :] for g in range(groups)]
+            columns.append(jnp.concatenate(parts, axis=0))
+            at = (comp * tiles + t) * modes + first
+            dense_ref[at : at + groups * 8, :] = columns[t]
+        at = slice(comp * modes + first, comp * modes + first + groups * 8)
+        for side, (lanes, tile) in enumerate(picks):
+            for g in range(groups):
+                value = jnp.zeros((8, LANES), jnp.float32)
+                for t in range(tiles):
+                    value = jnp.where(tile == t, lane_pick(columns[t][g * 8 : (g + 1) * 8], lanes), value)
+                outs[side][at.start + g * 8 : at.start + (g + 1) * 8, :] = value
+        whole = jnp.concatenate(columns, axis=1)
+        half = 96
+        for lo, hi in ((0, half), (half, groups * 8)):
+            rest = whole[lo:hi]
+            total = None
+            for s in range(3):
+                piece = rest.astype(jnp.bfloat16)
+                rest = rest - piece.astype(jnp.float32)
+                part = jnp.dot(piece, hot_ref[...], preferred_element_type=jnp.float32)
+                total = part if total is None else total + part
+            outs[2][at.start + lo : at.start + hi, :] = total[:, :LANES]
+            outs[3][at.start + lo : at.start + hi, :] = total[:, LANES:]
 
 
 def load(basis, send, modes):
     rows = basis.shape[0]
     tiles = rows // (3 * modes)
-    chunks = 6
+    chunks = CHUNKS
     shared = jax.ShapeDtypeStruct((3 * modes, LANES), jnp.float32)
+    basis = pltpu.with_memory_space_constraint(basis, pltpu.HBM)
+    send = pltpu.with_memory_space_constraint(send, pltpu.HBM)
     return pl.pallas_call(
         functools.partial(load_kernel, modes, tiles, chunks),
-        out_shape=(jax.ShapeDtypeStruct(basis.shape, jnp.float32), shared, shared),
-        in_specs=[HBM, VMEM],
-        out_specs=(VMEM,) * 3,
+        out_shape=(jax.ShapeDtypeStruct(basis.shape, jnp.float32),) + (shared,) * 4,
+        in_specs=[HBM, HBM],
+        out_specs=(VMEM,) * 5,
         scratch_shapes=[
             pltpu.VMEM((rows, LANES), jnp.float32),
+            pltpu.VMEM(send.shape, jnp.int32),
+            pltpu.VMEM((tiles * LANES, 2 * LANES), jnp.bfloat16),
             pltpu.SemaphoreType.DMA((chunks,)),
+            pltpu.SemaphoreType.DMA,
         ],
         compiler_params=pltpu.CompilerParams(vmem_limit_bytes=24 * MIB),
         name="load",
     )(basis, send)
 
 
-def share_kernel(modes, tiles, dense_ref, send_ref, below_ref, above_ref):
-    picks = picks_of(send_ref, (0, 1))
-
-    for c in range(3):
-
-        def body(g, carry, c=c):
-            read = [dense_ref[eight((c * tiles + t) * modes + g * 8), :] for t in range(tiles)]
-            for ref, value in zip((below_ref, above_ref), pick_rows(read, picks)):
-                ref[eight(c * modes + g * 8), :] = value
-            return carry
-
-        lax.fori_loop(0, modes // 8, body, 0, unroll=25)
-
-
-def share(dense, send, modes):
-    tiles = dense.shape[0] // (3 * modes)
-    shared = jax.ShapeDtypeStruct((3 * modes, LANES), jnp.float32)
-    return pl.pallas_call(
-        functools.partial(share_kernel, modes, tiles),
-        out_shape=(shared, shared),
-        in_specs=[VMEM, VMEM],
-        out_specs=(VMEM,) * 2,
-        compiler_params=pltpu.CompilerParams(vmem_limit_bytes=16 * MIB),
-        name="share",
-    )(dense, send)
+def edges():
+    x, y = lax.axis_index("gx"), lax.axis_index("gy")
+    return x > 0, x < lax.axis_size("gx") - 1, y > 0, y < lax.axis_size("gy") - 1
 
 
 def column(row):
@@ -198,6 +193,7 @@
         coords_out[...] = coords
         velocity_out[...] = velocity
     sides = (r0, r1, r2, r3)
+    present = edges()
     slots = tiles + 4
     elements = links_ref.shape[1]
     blocks = elements // LANES
@@ -212,7 +208,8 @@
         )
         owned, shared = rows[: 3 * tiles], rows[3 * tiles :]
     for c in range(3):
-        rows = owned[c * tiles : (c + 1) * tiles] + shared[c * 4 : (c + 1) * 4]
+        rows = owned[c * tiles : (c + 1) * tiles]
+        rows += [jnp.where(here, row, 0.0) for here, row in zip(present, shared[c * 4 : (c + 1) * 4])]
         for r, row in enumerate(rows):
             table[c * slots + r : c * slots + r + 1, :] = row
 
@@ -260,7 +257,7 @@
             if r < tiles:
                 places.append((dense_ref, (c * tiles + r) * modes, row))
             else:
-                places.append((sides[r - tiles], c * modes, row))
+                places.append((sides[r - tiles], c * modes, jnp.where(present[r - tiles], row, 0.0)))
 
     def body(k, carry):
         sums = [jnp.zeros((8, LANES), jnp.float32) for _ in range(3)]
@@ -336,7 +333,7 @@
 
 def exchange(below, above, axis):
     count = lax.axis_size(axis)
-    up = [(i, i + 1) for i in range(count - 1)]
+    up = [(i, (i + 1) % count) for i in range(count)]
     down = [(j, i) for i, j in up]
     return lax.ppermute(above, axis, up), lax.ppermute(below, axis, down)
 
@@ -354,11 +351,9 @@
     coords, velocity, external = (x[None, :] for x in (coords, velocity, external))
     devices = lax.axis_size("gx") * lax.axis_size("gy")
 
-    flat = pltpu.with_memory_space_constraint(flat, pltpu.HBM)
-    dense, below, above = load(flat, send_nodes, modes)
-    r2, r3 = exchange(below, above, "gy")
-    below, above = share(dense, send_nodes, modes)
-    r0, r1 = exchange(below, above, "gx")
+    dense, below_x, above_x, below_y, above_y = load(flat, send_nodes, modes)
+    r0, r1 = exchange(below_x, above_x, "gx")
+    r2, r3 = exchange(below_y, above_y, "gy")
     owned, low, high = prepare(dense, links, coords)
     sides = (r0, r1, r2, r3)
 

time: 77 us -> 75.2 us (0.977)
  waiting for transfers between devices: 8.06 us -> 11 us
  starting transfers between devices: 11.2 us -> 8.64 us
  Pallas kernels: 18.5 us -> 17.6 us
    pallas_call x1 -> x0, Pallas kernels: 3.59 us -> none  [share(): pl.pallas_call(functools.partial(share_kernel, modes, tiles), out_shape=(...]
    ppermute x4, waiting for transfers between devices: 8.06 us -> 11 us  [exchange(): return (lax.ppermute(above, axis, up), lax.ppermute(below, axis, down))]
    pallas_call x1, Pallas kernels: 4.89 us -> 7.5 us  [load(): pl.pallas_call(functools.partial(load_kernel, modes, tiles, chunks), out_...]
    ppermute x4, starting transfers between devices: 11.2 us -> 8.64 us  [exchange(): return (lax.ppermute(above, axis, up), lax.ppermute(below, axis, down))]
  transfers between devices with their start and end apart: 4 -> 4, of which waited for: 3 -> 2; matrix products, arithmetic and copies ran while one was open for 0% -> 0% of each run, Pallas kernels for 7% -> 2%
where the time goes in v3:
time: 75.2 us; the launch traced here: 75.1 us
  blocking collectives  37.1 us (49%)
  Pallas kernels  17.6 us (23%)
  waiting for transfers between devices  11 us (15%)
  starting transfers between devices  8.64 us (11%)
  between operations  0.76 us (1%)
    all_to_all x2, blocking collectives, everyone(): lax.all_to_all(chunks, ('gx', 'gy'), 0, 0, tiled=True).reshape(parts.shape)  37.1 us
    ppermute x4, waiting for transfers between devices, exchange(): return (lax.ppermute(above, axis, up), lax.ppermute(below, axis, down))  11 us
    ppermute x4, starting transfers between devices, exchange(): return (lax.ppermute(above, axis, up), lax.ppermute(below, axis, down))  8.64 us
    pallas_call x1, Pallas kernels, load(): pl.pallas_call(functools.partial(load_kernel, modes, tiles, chunks), out_...  7.5 us
    pallas_call x2, Pallas kernels, step(): pl.pallas_call(functools.partial(step_kernel, first, modes, tiles), out_s...  7.15 us
    pallas_call x1, Pallas kernels, finish(): pl.pallas_call(functools.partial(final_kernel, modes, tiles), out_shape=(...  1.51 us
  transfers between devices with their start and end apart: 4, of which 2 were waited for; matrix products, arithmetic and copies ran while one was open for 0% of the time, Pallas kernels for 2%

profile of v3, /device:TPU:1, one launch (start us, length us, event | category | flops | bytes accessed | tf_op | source)
XLA Modules:
  0.0 75.1 jit_solution(9065878469950825383)
XLA Ops:
  0.6 0.0 copy-start.6
  0.6 0.0 copy-start.1
  0.7 0.0 copy-start
  0.7 0.0 copy-start.2
  0.7 0.0 copy-start.3
  0.7 7.5 %load.1 = (f32[12000,128]{1,0:T(8,128)S(1)}, f32[1200,128]{1,0:T(8,128)S(1)}, f32[1200,128]{1,0:T(8,128)S(1)}, f32[1200,128]{1,0:T(8,128)S(1)}, f32[1200,128]{1,0:T(8,128)S(1)}) custom-call(f32[12000,128]{1,0:T(8,128)} %bitcast.27, s32[4,1,128]{2,1,0:T(1,128)} %send_hbm.1), custom_call_target="tpu_custom_call" | custom-call | tf_op jit(solution)/shard_map/load/pallas_call | solution.py:95
  8.2 2.7 %collective-permute-start = (f32[1200,128]{1,0:T(8,128)S(1)}, f32[1200,128]{1,0:T(8,128)S(1)}, u32[]{:S(2)}, u32[]{:S(2)}) collective-permute-start(f32[1200,128]{1,0:T(8,128)S(1)} %get-tuple-element.21), channel_id=1, source_target_pairs={{0,16},{16,32},{32,48},{48,64},{64,80},{80,96},{96,112},{112,0},{1... | collective-permute-start | bytes 1843208 | tf_op jit(solution)/shard_map/ppermute | solution.py:338
  10.9 0.0 collective-permute-start.1
  10.9 1.2 %collective-permute-start.2 = (f32[1200,128]{1,0:T(8,128)S(1)}, f32[1200,128]{1,0:T(8,128)S(1)}, u32[]{:S(2)}, u32[]{:S(2)}) collective-permute-start(f32[1200,128]{1,0:T(8,128)S(1)} %get-tuple-element.23), channel_id=1, source_target_pairs={{0,1},{1,2},{2,3},{3,4},{4,5},{5,6},{6,7},{7,8},{8,9},{9,10},{10,1... | collective-permute-start | bytes 1843208 | tf_op jit(solution)/shard_map/ppermute | solution.py:338
  12.1 4.7 %collective-permute-start.3 = (f32[1200,128]{1,0:T(8,128)S(1)}, f32[1200,128]{1,0:T(8,128)S(1)}, u32[]{:S(2)}, u32[]{:S(2)}) collective-permute-start(f32[1200,128]{1,0:T(8,128)S(1)} %get-tuple-element.24), channel_id=1, source_target_pairs={{1,0},{2,1},{3,2},{4,3},{5,4},{6,5},{7,6},{8,7},{9,8},{10,9},{11,1... | collective-permute-start | bytes 1843208 | tf_op jit(solution)/shard_map/ppermute | solution.py:338
  16.8 0.0 copy-done.6
  16.8 0.0 copy-done.1
  16.9 1.4 %prepare.1 = (f32[32,128]{1,0:T(8,128)S(1)}, bf16[128,8192]{1,0:T(8,128)(2,1)S(1)}, bf16[16,8192]{1,0:T(8,128)(2,1)S(1)}) custom-call(f32[12000,128]{1,0:T(8,128)S(1)} %get-tuple-element.19.dense_ref.refs_1_, s32[8,1024]{1,0:T(8,128)S(1)} %bitcast.17, f32[1,400]{1,0:T(1,128)S(1)} %bitcast.21), custom_call_target="tpu_custom_call" | custom-call | tf_op jit(solution)/shard_map/prepare/pallas_call | solution.py:158
  18.3 0.0 copy-start.4
  18.3 0.0 copy-start.5
  18.3 0.0 collective-permute-done.refs_2_
  18.3 2.4 %collective-permute-done.1.refs_3_ = f32[1200,128]{1,0:T(8,128)S(1)} collective-permute-done((f32[1200,128]{1,0:T(8,128)S(1)}, f32[1200,128]{1,0:T(8,128)S(1)}, u32[]{:S(2)}, u32[]{:S(2)}) %collective-permute-start.1) | collective-permute-done | bytes 614432 | tf_op jit(solution)/shard_map/ppermute | solution.py:338
  20.7 8.5 %collective-permute-done.2.refs_4_ = f32[1200,128]{1,0:T(8,128)S(1)} collective-permute-done((f32[1200,128]{1,0:T(8,128)S(1)}, f32[1200,128]{1,0:T(8,128)S(1)}, u32[]{:S(2)}, u32[]{:S(2)}) %collective-permute-start.2) | collective-permute-done | bytes 614432 | tf_op jit(solution)/shard_map/ppermute | solution.py:338
  29.3 0.0 collective-permute-done.3.refs_5_
  29.3 0.0 copy-done
  29.3 0.0 copy-done.2
  29.3 0.0 copy-done.3
  29.3 3.2 %first_step.1 = f32[512,128]{1,0:T(8,128)S(1)} custom-call(f32[32,128]{1,0:T(8,128)S(1)} %get-tuple-element.20.refs_0_, f32[12000,128]{1,0:T(8,128)S(1)} %get-tuple-element.19.dense_ref.refs_1_, f32[1200,128]{1,0:T(8,128)S(1)} %collective-permute-done.refs_2_, f32[1200,128]{1,0:T(8,128)S(1)} %collective-permute-done.1.refs_3_, ...), custom_call_target="tpu_custom_call" | custom-call | tf_op jit(solution)/shard_map/first_step/pallas_call | solution.py:290
  32.6 21.9 %all_to_all.10 = f32[128,4,128]{2,1,0:T(4,128)S(1)} all-to-all(f32[128,4,128]{2,1,0:T(4,128)S(1)} %bitcast.16), channel_id=1, replica_groups=mesh['gx'=8,'gy'=16] {'gx','gy'}, dimensions={0} | all-to-all | bytes 524288 | tf_op jit(solution)/shard_map/all_to_all | solution.py:343
  54.4 0.0 copy-done.4
  54.4 0.0 copy-done.5
  54.4 3.9 %next_step.1 = (f32[512,128]{1,0:T(8,128)S(1)}, f32[1,400]{1,0:T(1,128)S(1)}, f32[1,400]{1,0:T(1,128)S(1)}) custom-call(f32[512,128]{1,0:T(8,128)S(1)} %bitcast.14, f32[12000,128]{1,0:T(8,128)S(1)} %get-tuple-element.19.dense_ref.refs_1_, f32[1200,128]{1,0:T(8,128)S(1)} %collective-permute-done.refs_2_, f32[1200,128]{1,0:T(8,128)S(1)} %collective-permute-done.1.refs_3_, ...), custom_call_target="tpu_custom_call" | custom-call | tf_op jit(solution)/shard_map/next_step/pallas_call | solution.py:290
  58.3 15.2 %all_to_all.11 = f32[128,4,128]{2,1,0:T(4,128)S(1)} all-to-all(f32[128,4,128]{2,1,0:T(4,128)S(1)} %bitcast.20), channel_id=1, replica_groups=mesh['gx'=8,'gy'=16] {'gx','gy'}, dimensions={0} | all-to-all | bytes 524288 | tf_op jit(solution)/shard_map/all_to_all | solution.py:343
  73.6 1.5 %finish.1 = (f32[1,400]{1,0:T(1,128)}, f32[1,400]{1,0:T(1,128)}, f32[1,400]{1,0:T(1,128)}, f32[3,1,1280]{2,1,0:T(1,128)}) custom-call(f32[512,128]{1,0:T(8,128)S(1)} %bitcast.15, f32[12000,128]{1,0:T(8,128)S(1)} %get-tuple-element.19.dense_ref.refs_1_, f32[1,400]{1,0:T(1,128)S(1)} %get-tuple-element.28.coords_ref, ...), custom_call_target="tpu_custom_call" | custom-call | tf_op jit(solution)/shard_map/finish/pallas_call | solution.py:323
  (1 shorter events, 0.0 us)
Async XLA Ops:
  0.6 16.2 %copy-start.6 = (s32[8,1,1024]{2,1,0:T(1,128)S(1)}, s32[8,1,1024]{2,1,0:T(1,128)}, u32[]{:S(2)}) copy-start(s32[8,1,1024]{2,1,0:T(1,128)} %param.10) | copy-start | bytes 98308
  0.6 16.2 %copy-start.1 = (f32[400]{0:T(512)S(1)}, f32[400]{0:T(512)}, u32[]{:S(2)}) copy-start(f32[400]{0:T(512)} %param.15) | copy-start | bytes 4804
  0.7 28.6 %copy-start = (f32[24,24]{1,0:T(8,128)S(1)}, f32[24,24]{1,0:T(8,128)}, u32[]{:S(2)}) copy-start(f32[24,24]{1,0:T(8,128)} %refs_11_.3) | copy-start | bytes 6916
  0.7 28.6 %copy-start.2 = (f32[1,1024]{1,0:T(1,128)S(1)}, f32[1,1024]{1,0:T(1,128)}, u32[]{:S(2)}) copy-start(f32[1,1024]{1,0:T(1,128)} %refs_9_.3) | copy-start | bytes 12292
  0.7 28.6 %copy-start.3 = (f32[1,1024]{1,0:T(1,128)S(1)}, f32[1,1024]{1,0:T(1,128)}, u32[]{:S(2)}) copy-start(f32[1,1024]{1,0:T(1,128)} %refs_10_.3) | copy-start | bytes 12292
  8.2 10.1 %collective-permute-start = (f32[1200,128]{1,0:T(8,128)S(1)}, f32[1200,128]{1,0:T(8,128)S(1)}, u32[]{:S(2)}, u32[]{:S(2)}) collective-permute-start(f32[1200,128]{1,0:T(8,128)S(1)} %get-tuple-element.21), channel_id=1, source_target_pairs={{0,16},{16,32},{32,48},{48,64},{64,80},{80,96},{96,112},{112,0},{1... | collective-permute-start | bytes 1843208 | tf_op jit(solution)/shard_map/ppermute | solution.py:338
  10.9 9.9 %collective-permute-start.1 = (f32[1200,128]{1,0:T(8,128)S(1)}, f32[1200,128]{1,0:T(8,128)S(1)}, u32[]{:S(2)}, u32[]{:S(2)}) collective-permute-start(f32[1200,128]{1,0:T(8,128)S(1)} %get-tuple-element.22), channel_id=1, source_target_pairs={{16,0},{32,16},{48,32},{64,48},{80,64},{96,80},{112,96},{0,112},{1... | collective-permute-start | bytes 1843208 | tf_op jit(solution)/shard_map/ppermute | solution.py:338
  10.9 18.4 %collective-permute-start.2 = (f32[1200,128]{1,0:T(8,128)S(1)}, f32[1200,128]{1,0:T(8,128)S(1)}, u32[]{:S(2)}, u32[]{:S(2)}) collective-permute-start(f32[1200,128]{1,0:T(8,128)S(1)} %get-tuple-element.23), channel_id=1, source_target_pairs={{0,1},{1,2},{2,3},{3,4},{4,5},{5,6},{6,7},{7,8},{8,9},{9,10},{10,1... | collective-permute-start | bytes 1843208 | tf_op jit(solution)/shard_map/ppermute | solution.py:338
  12.1 17.2 %collective-permute-start.3 = (f32[1200,128]{1,0:T(8,128)S(1)}, f32[1200,128]{1,0:T(8,128)S(1)}, u32[]{:S(2)}, u32[]{:S(2)}) collective-permute-start(f32[1200,128]{1,0:T(8,128)S(1)} %get-tuple-element.24), channel_id=1, source_target_pairs={{1,0},{2,1},{3,2},{4,3},{5,4},{6,5},{7,6},{8,7},{9,8},{10,9},{11,1... | collective-permute-start | bytes 1843208 | tf_op jit(solution)/shard_map/ppermute | solution.py:338
  18.3 36.1 %copy-start.4 = (f32[400]{0:T(512)S(1)}, f32[400]{0:T(512)}, u32[]{:S(2)}) copy-start(f32[400]{0:T(512)} %param.17) | copy-start | bytes 4804
  18.3 36.1 %copy-start.5 = (f32[400]{0:T(512)S(1)}, f32[400]{0:T(512)}, u32[]{:S(2)}) copy-start(f32[400]{0:T(512)} %param.16) | copy-start | bytes 4804

commit v4 on v3

--- a/solution.py
+++ b/solution.py
@@ -11,7 +11,8 @@
 DT = 0.05
 LANES = 128
 SPLITS = 3
-CHUNKS = 6
+PIECES = 2
+BOUNDS = (0, 400)
 MIB = 2**20
 
 VMEM = pl.BlockSpec(memory_space=pltpu.VMEM)
@@ -26,25 +27,18 @@
     return pl.ds(pl.multiple_of(start, 8), 8)
 
 
-def load_kernel(modes, tiles, chunks, basis_ref, send_hbm, dense_ref, *refs):
-    outs, (buf, send_ref, hot_ref, sems, send_sem) = refs[:4], refs[4:]
-    size = buf.shape[0] // chunks
-    copies = [
-        pltpu.make_async_copy(
-            basis_ref.at[pl.ds(i * size, size)], buf.at[pl.ds(i * size, size)], sems.at[i]
-        )
-        for i in range(chunks)
-    ]
+def load_kernel(modes, tiles, bounds, basis_ref, send_hbm, buf, *refs):
+    outs, (send_ref, hot_ref, piece_ref, sems, send_sem) = refs[:4], refs[4:]
+    chunks = [(c, lo, hi) for c in range(3) for lo, hi in zip(bounds, bounds[1:])]
+    copies = []
+    for i, (c, lo, hi) in enumerate(chunks):
+        part = pl.ds((c * modes + lo) * tiles, (hi - lo) * tiles)
+        copies.append(pltpu.make_async_copy(basis_ref.at[part], buf.at[part], sems.at[i]))
     lists = pltpu.make_async_copy(send_hbm, send_ref, send_sem)
     lists.start()
     for copy in copies:
         copy.start()
     lists.wait()
-
-    picks = []
-    for side in range(2):
-        nodes = jnp.broadcast_to(send_ref[side], (8, LANES))
-        picks.append((nodes & (LANES - 1), nodes >> 7))
     for t in range(tiles):
         count = lax.broadcasted_iota(jnp.int32, (LANES, LANES), 0) + t * LANES
         for side in range(2):
@@ -52,59 +46,74 @@
             hot_ref[t * LANES : (t + 1) * LANES, side * LANES : (side + 1) * LANES] = jnp.where(
                 hot, 1.0, 0.0
             ).astype(jnp.bfloat16)
-
-    groups = size // (8 * tiles)
-    per = chunks // 3
-    for i in range(chunks):
+    picks = []
+    for side in range(2):
+        nodes = jnp.broadcast_to(send_ref[side], (8, LANES))
+        picks.append((nodes & (LANES - 1), nodes >> 7))
+
+    def split(i):
+        c, lo, hi = chunks[i]
         copies[i].wait()
-        comp, first = i // per, (i % per) * groups * 8
-        columns = []
-        for t in range(tiles):
-            parts = [buf[pl.ds((i * groups + g) * 8 * tiles + t, 8, stride=tiles), :] for g in range(groups)]
-            columns.append(jnp.concatenate(parts, axis=0))
-            at = (comp * tiles + t) * modes + first
-            dense_ref[at : at + groups * 8, :] = columns[t]
-        at = slice(comp * modes + first, comp * modes + first + groups * 8)
-        for side, (lanes, tile) in enumerate(picks):
-            for g in range(groups):
-                value = jnp.zeros((8, LANES), jnp.float32)
-                for t in range(tiles):
-                    value = jnp.where(tile == t, lane_pick(columns[t][g * 8 : (g + 1) * 8], lanes), value)
-                outs[side][at.start + g * 8 : at.start + (g + 1) * 8, :] = value
-        whole = jnp.concatenate(columns, axis=1)
-        half = 96
-        for lo, hi in ((0, half), (half, groups * 8)):
-            rest = whole[lo:hi]
-            total = None
-            for s in range(3):
-                piece = rest.astype(jnp.bfloat16)
-                rest = rest - piece.astype(jnp.float32)
-                part = jnp.dot(piece, hot_ref[...], preferred_element_type=jnp.float32)
-                total = part if total is None else total + part
-            outs[2][at.start + lo : at.start + hi, :] = total[:, :LANES]
-            outs[3][at.start + lo : at.start + hi, :] = total[:, LANES:]
+        for m in range(lo, hi, 16):
+            for t in range(tiles):
+                at = (c * modes + m) * tiles + t
+                rows = [buf[pl.ds(at + 8 * tiles * h, 8, stride=tiles), :] for h in range(2)]
+                rest = jnp.concatenate(rows, axis=0)
+                for s in range(PIECES):
+                    piece = rest.astype(jnp.bfloat16)
+                    piece_ref[s, c * modes + m : c * modes + m + 16, t * LANES : (t + 1) * LANES] = piece
+                    if s + 1 < PIECES:
+                        rest = rest - piece.astype(jnp.float32)
+
+    def pick(i):
+        c, lo, hi = chunks[i]
+        at = slice(c * modes + lo, c * modes + hi)
+        total = None
+        for s in range(PIECES):
+            part = jnp.dot(piece_ref[s, at, :], hot_ref[...], preferred_element_type=jnp.float32)
+            total = part if total is None else total + part
+        outs[2][at, :] = total[:, :LANES]
+        outs[3][at, :] = total[:, LANES:]
+
+    def permute(i):
+        c, lo, hi = chunks[i]
+        for m in range(c * modes + lo, c * modes + hi, 8):
+            sums = [jnp.zeros((8, LANES), jnp.float32) for _ in range(2)]
+            for t in range(tiles):
+                rows = buf[pl.ds(m * tiles + t, 8, stride=tiles), :]
+                for side, (lanes, tile) in enumerate(picks):
+                    sums[side] = jnp.where(tile == t, lane_pick(rows, lanes), sums[side])
+            for side in range(2):
+                outs[side][m : m + 8, :] = sums[side]
+
+    split(0)
+    for i in range(len(chunks)):
+        permute(i)
+        pick(i)
+        if i + 1 < len(chunks):
+            split(i + 1)
 
 
 def load(basis, send, modes):
     rows = basis.shape[0]
     tiles = rows // (3 * modes)
-    chunks = CHUNKS
+    bounds = BOUNDS
     shared = jax.ShapeDtypeStruct((3 * modes, LANES), jnp.float32)
     basis = pltpu.with_memory_space_constraint(basis, pltpu.HBM)
     send = pltpu.with_memory_space_constraint(send, pltpu.HBM)
     return pl.pallas_call(
-        functools.partial(load_kernel, modes, tiles, chunks),
+        functools.partial(load_kernel, modes, tiles, bounds),
         out_shape=(jax.ShapeDtypeStruct(basis.shape, jnp.float32),) + (shared,) * 4,
         in_specs=[HBM, HBM],
         out_specs=(VMEM,) * 5,
         scratch_shapes=[
-            pltpu.VMEM((rows, LANES), jnp.float32),
             pltpu.VMEM(send.shape, jnp.int32),
             pltpu.VMEM((tiles * LANES, 2 * LANES), jnp.bfloat16),
-            pltpu.SemaphoreType.DMA((chunks,)),
+            pltpu.VMEM((PIECES, 3 * modes, tiles * LANES), jnp.bfloat16),
+            pltpu.SemaphoreType.DMA((3 * (len(bounds) - 1),)),
             pltpu.SemaphoreType.DMA,
         ],
-        compiler_params=pltpu.CompilerParams(vmem_limit_bytes=24 * MIB),
+        compiler_params=pltpu.CompilerParams(vmem_limit_bytes=32 * MIB),
         name="load",
     )(basis, send)
 
@@ -118,10 +127,17 @@
     return jnp.transpose(jnp.broadcast_to(row, (LANES, row.shape[1])))
 
 
+def rows_of(place, k):
+    ref, at, stride = place
+    if stride == 1:
+        return ref[eight(at + k * 8), :]
+    return ref[pl.ds(at + k * (8 * stride), 8, stride=stride), :]
+
+
 def contract(places, cols, modes):
     def body(k, sums):
         scale = cols[eight(k * 8), :]
-        return tuple(s + ref[eight(at + k * 8), :] * scale for s, (ref, at) in zip(sums, places))
+        return tuple(s + rows_of(place, k) * scale for s, place in zip(sums, places))
 
     zero = jnp.zeros((8, LANES), jnp.float32)
     sums = lax.fori_loop(0, modes // 8, body, (zero,) * len(places), unroll=2)
@@ -129,11 +145,11 @@
 
 
 def owned_places(dense_ref, modes, tiles):
-    return [(dense_ref, (c * tiles + t) * modes) for c in range(3) for t in range(tiles)]
+    return [(dense_ref, c * modes * tiles + t, tiles) for c in range(3) for t in range(tiles)]
 
 
 def shared_places(sides, modes):
-    return [(side, c * modes) for c in range(3) for side in sides]
+    return [(side, c * modes, 1) for c in range(3) for side in sides]
 
 
 def prepare_kernel(modes, tiles, dense_ref, links_ref, coords_ref, owned_ref, low_ref, high_ref, cols):
@@ -255,14 +271,14 @@
         for r in range(slots):
             row = jnp.broadcast_to(total[c * 16 + r : c * 16 + r + 1], (8, LANES))
             if r < tiles:
-                places.append((dense_ref, (c * tiles + r) * modes, row))
+                places.append(((dense_ref, c * modes * tiles + r, tiles), row))
             else:
-                places.append((sides[r - tiles], c * modes, jnp.where(present[r - tiles], row, 0.0)))
+                places.append(((sides[r - tiles], c * modes, 1), jnp.where(present[r - tiles], row, 0.0)))
 
     def body(k, carry):
         sums = [jnp.zeros((8, LANES), jnp.float32) for _ in range(3)]
-        for i, (ref, at, row) in enumerate(places):
-            sums[i % 3] = sums[i % 3] + ref[eight(at + k * 8), :] * row
+        for i, (place, row) in enumerate(places):
+            sums[i % 3] = sums[i % 3] + rows_of(place, k) * row
         cols[eight(k * 8), :] = sums[0] + sums[1] + sums[2]
         return carry
 

time: 75.2 us -> 73.4 us (0.976)
  Pallas kernels: 17.6 us -> 15.8 us
    pallas_call x1, Pallas kernels: 7.5 us -> 5.7 us  [load(): pl.pallas_call(functools.partial(load_kernel, modes, tiles, bounds), out_...]
where the time goes in v4:
time: 73.4 us; the launch traced here: 73.3 us
  blocking collectives  37.1 us (51%)
  Pallas kernels  15.8 us (22%)
  waiting for transfers between devices  11 us (15%)
  starting transfers between devices  8.63 us (12%)
  between operations  0.76 us (1%)
    all_to_all x2, blocking collectives, everyone(): lax.all_to_all(chunks, ('gx', 'gy'), 0, 0, tiled=True).reshape(parts.shape)  37.1 us
    ppermute x4, waiting for transfers between devices, exchange(): return (lax.ppermute(above, axis, up), lax.ppermute(below, axis, down))  11 us
    ppermute x4, starting transfers between devices, exchange(): return (lax.ppermute(above, axis, up), lax.ppermute(below, axis, down))  8.63 us
    pallas_call x2, Pallas kernels, step(): pl.pallas_call(functools.partial(step_kernel, first, modes, tiles), out_s...  7.16 us
    pallas_call x1, Pallas kernels, load(): pl.pallas_call(functools.partial(load_kernel, modes, tiles, bounds), out_...  5.7 us
    pallas_call x1, Pallas kernels, finish(): pl.pallas_call(functools.partial(final_kernel, modes, tiles), out_shape=(...  1.51 us
  transfers between devices with their start and end apart: 4, of which 2 were waited for; matrix products, arithmetic and copies ran while one was open for 0% of the time, Pallas kernels for 2%

profile of v4, /device:TPU:1, one launch (start us, length us, event | category | flops | bytes accessed | tf_op | source)
XLA Modules:
  0.0 73.3 jit_solution(9285881064388701511)
XLA Ops:
  0.6 0.0 copy-start.6
  0.6 0.0 copy-start.1
  0.7 0.0 copy-start
  0.7 0.0 copy-start.2
  0.7 0.0 copy-start.3
  0.7 5.7 %load.1 = (f32[12000,128]{1,0:T(8,128)S(1)}, f32[1200,128]{1,0:T(8,128)S(1)}, f32[1200,128]{1,0:T(8,128)S(1)}, f32[1200,128]{1,0:T(8,128)S(1)}, f32[1200,128]{1,0:T(8,128)S(1)}) custom-call(f32[12000,128]{1,0:T(8,128)} %bitcast.27, s32[4,1,128]{2,1,0:T(1,128)} %send_hbm.1), custom_call_target="tpu_custom_call" | custom-call | tf_op jit(solution)/shard_map/load/pallas_call | solution.py:104
  6.4 2.7 %collective-permute-start = (f32[1200,128]{1,0:T(8,128)S(1)}, f32[1200,128]{1,0:T(8,128)S(1)}, u32[]{:S(2)}, u32[]{:S(2)}) collective-permute-start(f32[1200,128]{1,0:T(8,128)S(1)} %get-tuple-element.21), channel_id=1, source_target_pairs={{0,16},{16,32},{32,48},{48,64},{64,80},{80,96},{96,112},{112,0},{1... | collective-permute-start | bytes 1843208 | tf_op jit(solution)/shard_map/ppermute | solution.py:354
  9.1 0.0 collective-permute-start.1
  9.1 1.2 %collective-permute-start.2 = (f32[1200,128]{1,0:T(8,128)S(1)}, f32[1200,128]{1,0:T(8,128)S(1)}, u32[]{:S(2)}, u32[]{:S(2)}) collective-permute-start(f32[1200,128]{1,0:T(8,128)S(1)} %get-tuple-element.23), channel_id=1, source_target_pairs={{0,1},{1,2},{2,3},{3,4},{4,5},{5,6},{6,7},{7,8},{8,9},{9,10},{10,1... | collective-permute-start | bytes 1843208 | tf_op jit(solution)/shard_map/ppermute | solution.py:354
  10.3 4.7 %collective-permute-start.3 = (f32[1200,128]{1,0:T(8,128)S(1)}, f32[1200,128]{1,0:T(8,128)S(1)}, u32[]{:S(2)}, u32[]{:S(2)}) collective-permute-start(f32[1200,128]{1,0:T(8,128)S(1)} %get-tuple-element.24), channel_id=1, source_target_pairs={{1,0},{2,1},{3,2},{4,3},{5,4},{6,5},{7,6},{8,7},{9,8},{10,9},{11,1... | collective-permute-start | bytes 1843208 | tf_op jit(solution)/shard_map/ppermute | solution.py:354
  15.0 0.0 copy-done.6
  15.0 0.0 copy-done.1
  15.1 1.4 %prepare.1 = (f32[32,128]{1,0:T(8,128)S(1)}, bf16[128,8192]{1,0:T(8,128)(2,1)S(1)}, bf16[16,8192]{1,0:T(8,128)(2,1)S(1)}) custom-call(f32[12000,128]{1,0:T(8,128)S(1)} %get-tuple-element.19.dense_ref.refs_1_, s32[8,1024]{1,0:T(8,128)S(1)} %bitcast.17, f32[1,400]{1,0:T(1,128)S(1)} %bitcast.21), custom_call_target="tpu_custom_call" | custom-call | tf_op jit(solution)/shard_map/prepare/pallas_call | solution.py:174
  16.5 0.0 copy-start.4
  16.5 0.0 copy-start.5
  16.5 0.0 collective-permute-done.refs_2_
  16.5 2.4 %collective-permute-done.1.refs_3_ = f32[1200,128]{1,0:T(8,128)S(1)} collective-permute-done((f32[1200,128]{1,0:T(8,128)S(1)}, f32[1200,128]{1,0:T(8,128)S(1)}, u32[]{:S(2)}, u32[]{:S(2)}) %collective-permute-start.1) | collective-permute-done | bytes 614432 | tf_op jit(solution)/shard_map/ppermute | solution.py:354
  18.9 8.5 %collective-permute-done.2.refs_4_ = f32[1200,128]{1,0:T(8,128)S(1)} collective-permute-done((f32[1200,128]{1,0:T(8,128)S(1)}, f32[1200,128]{1,0:T(8,128)S(1)}, u32[]{:S(2)}, u32[]{:S(2)}) %collective-permute-start.2) | collective-permute-done | bytes 614432 | tf_op jit(solution)/shard_map/ppermute | solution.py:354
  27.5 0.0 collective-permute-done.3.refs_5_
  27.5 0.0 copy-done
  27.5 0.0 copy-done.2
  27.5 0.0 copy-done.3
  27.5 3.3 %first_step.1 = f32[512,128]{1,0:T(8,128)S(1)} custom-call(f32[32,128]{1,0:T(8,128)S(1)} %get-tuple-element.20.refs_0_, f32[12000,128]{1,0:T(8,128)S(1)} %get-tuple-element.19.dense_ref.refs_1_, f32[1200,128]{1,0:T(8,128)S(1)} %collective-permute-done.refs_2_, f32[1200,128]{1,0:T(8,128)S(1)} %collective-permute-done.1.refs_3_, ...), custom_call_target="tpu_custom_call" | custom-call | tf_op jit(solution)/shard_map/first_step/pallas_call | solution.py:306
  30.8 21.9 %all_to_all.10 = f32[128,4,128]{2,1,0:T(4,128)S(1)} all-to-all(f32[128,4,128]{2,1,0:T(4,128)S(1)} %bitcast.16), channel_id=1, replica_groups=mesh['gx'=8,'gy'=16] {'gx','gy'}, dimensions={0} | all-to-all | bytes 524288 | tf_op jit(solution)/shard_map/all_to_all | solution.py:359
  52.6 0.0 copy-done.4
  52.6 0.0 copy-done.5
  52.6 3.9 %next_step.1 = (f32[512,128]{1,0:T(8,128)S(1)}, f32[1,400]{1,0:T(1,128)S(1)}, f32[1,400]{1,0:T(1,128)S(1)}) custom-call(f32[512,128]{1,0:T(8,128)S(1)} %bitcast.14, f32[12000,128]{1,0:T(8,128)S(1)} %get-tuple-element.19.dense_ref.refs_1_, f32[1200,128]{1,0:T(8,128)S(1)} %collective-permute-done.refs_2_, f32[1200,128]{1,0:T(8,128)S(1)} %collective-permute-done.1.refs_3_, ...), custom_call_target="tpu_custom_call" | custom-call | tf_op jit(solution)/shard_map/next_step/pallas_call | solution.py:306
  56.5 15.2 %all_to_all.11 = f32[128,4,128]{2,1,0:T(4,128)S(1)} all-to-all(f32[128,4,128]{2,1,0:T(4,128)S(1)} %bitcast.20), channel_id=1, replica_groups=mesh['gx'=8,'gy'=16] {'gx','gy'}, dimensions={0} | all-to-all | bytes 524288 | tf_op jit(solution)/shard_map/all_to_all | solution.py:359
  71.8 1.5 %finish.1 = (f32[1,400]{1,0:T(1,128)}, f32[1,400]{1,0:T(1,128)}, f32[1,400]{1,0:T(1,128)}, f32[3,1,1280]{2,1,0:T(1,128)}) custom-call(f32[512,128]{1,0:T(8,128)S(1)} %bitcast.15, f32[12000,128]{1,0:T(8,128)S(1)} %get-tuple-element.19.dense_ref.refs_1_, f32[1,400]{1,0:T(1,128)S(1)} %get-tuple-element.28.coords_ref, ...), custom_call_target="tpu_custom_call" | custom-call | tf_op jit(solution)/shard_map/finish/pallas_call | solution.py:339
  (1 shorter events, 0.0 us)
Async XLA Ops:
  0.6 14.4 %copy-start.6 = (s32[8,1,1024]{2,1,0:T(1,128)S(1)}, s32[8,1,1024]{2,1,0:T(1,128)}, u32[]{:S(2)}) copy-start(s32[8,1,1024]{2,1,0:T(1,128)} %param.10) | copy-start | bytes 98308
  0.6 14.4 %copy-start.1 = (f32[400]{0:T(512)S(1)}, f32[400]{0:T(512)}, u32[]{:S(2)}) copy-start(f32[400]{0:T(512)} %param.15) | copy-start | bytes 4804
  0.7 26.8 %copy-start = (f32[24,24]{1,0:T(8,128)S(1)}, f32[24,24]{1,0:T(8,128)}, u32[]{:S(2)}) copy-start(f32[24,24]{1,0:T(8,128)} %refs_11_.3) | copy-start | bytes 6916
  0.7 26.8 %copy-start.2 = (f32[1,1024]{1,0:T(1,128)S(1)}, f32[1,1024]{1,0:T(1,128)}, u32[]{:S(2)}) copy-start(f32[1,1024]{1,0:T(1,128)} %refs_9_.3) | copy-start | bytes 12292
  0.7 26.8 %copy-start.3 = (f32[1,1024]{1,0:T(1,128)S(1)}, f32[1,1024]{1,0:T(1,128)}, u32[]{:S(2)}) copy-start(f32[1,1024]{1,0:T(1,128)} %refs_10_.3) | copy-start | bytes 12292
  6.4 10.1 %collective-permute-start = (f32[1200,128]{1,0:T(8,128)S(1)}, f32[1200,128]{1,0:T(8,128)S(1)}, u32[]{:S(2)}, u32[]{:S(2)}) collective-permute-start(f32[1200,128]{1,0:T(8,128)S(1)} %get-tuple-element.21), channel_id=1, source_target_pairs={{0,16},{16,32},{32,48},{48,64},{64,80},{80,96},{96,112},{112,0},{1... | collective-permute-start | bytes 1843208 | tf_op jit(solution)/shard_map/ppermute | solution.py:354
  9.1 9.9 %collective-permute-start.1 = (f32[1200,128]{1,0:T(8,128)S(1)}, f32[1200,128]{1,0:T(8,128)S(1)}, u32[]{:S(2)}, u32[]{:S(2)}) collective-permute-start(f32[1200,128]{1,0:T(8,128)S(1)} %get-tuple-element.22), channel_id=1, source_target_pairs={{16,0},{32,16},{48,32},{64,48},{80,64},{96,80},{112,96},{0,112},{1... | collective-permute-start | bytes 1843208 | tf_op jit(solution)/shard_map/ppermute | solution.py:354
  9.1 18.4 %collective-permute-start.2 = (f32[1200,128]{1,0:T(8,128)S(1)}, f32[1200,128]{1,0:T(8,128)S(1)}, u32[]{:S(2)}, u32[]{:S(2)}) collective-permute-start(f32[1200,128]{1,0:T(8,128)S(1)} %get-tuple-element.23), channel_id=1, source_target_pairs={{0,1},{1,2},{2,3},{3,4},{4,5},{5,6},{6,7},{7,8},{8,9},{9,10},{10,1... | collective-permute-start | bytes 1843208 | tf_op jit(solution)/shard_map/ppermute | solution.py:354
  10.3 17.2 %collective-permute-start.3 = (f32[1200,128]{1,0:T(8,128)S(1)}, f32[1200,128]{1,0:T(8,128)S(1)}, u32[]{:S(2)}, u32[]{:S(2)}) collective-permute-start(f32[1200,128]{1,0:T(8,128)S(1)} %get-tuple-element.24), channel_id=1, source_target_pairs={{1,0},{2,1},{3,2},{4,3},{5,4},{6,5},{7,6},{8,7},{9,8},{10,9},{11,1... | collective-permute-start | bytes 1843208 | tf_op jit(solution)/shard_map/ppermute | solution.py:354
  16.5 36.2 %copy-start.4 = (f32[400]{0:T(512)S(1)}, f32[400]{0:T(512)}, u32[]{:S(2)}) copy-start(f32[400]{0:T(512)} %param.17) | copy-start | bytes 4804
  16.5 36.1 %copy-start.5 = (f32[400]{0:T(512)S(1)}, f32[400]{0:T(512)}, u32[]{:S(2)}) copy-start(f32[400]{0:T(512)} %param.16) | copy-start | bytes 4804

commit v5 on v4

--- a/solution.py
+++ b/solution.py
@@ -7,12 +7,12 @@
 from jax.experimental.pallas import tpu as pltpu
 from jax.sharding import PartitionSpec as P
 
+
 STEPS = 2
 DT = 0.05
 LANES = 128
-SPLITS = 3
+SPLITS = 2
 PIECES = 2
-BOUNDS = (0, 400)
 MIB = 2**20
 
 VMEM = pl.BlockSpec(memory_space=pltpu.VMEM)
@@ -27,13 +27,13 @@
     return pl.ds(pl.multiple_of(start, 8), 8)
 
 
-def load_kernel(modes, tiles, bounds, basis_ref, send_hbm, buf, *refs):
-    outs, (send_ref, hot_ref, piece_ref, sems, send_sem) = refs[:4], refs[4:]
-    chunks = [(c, lo, hi) for c in range(3) for lo, hi in zip(bounds, bounds[1:])]
+def load_kernel(modes, tiles, basis_ref, send_hbm, buf, piece_ref, hot_ref, below_ref, above_ref,
+                send_ref, hot_y, sems, send_sem):
+    size = modes * tiles
     copies = []
-    for i, (c, lo, hi) in enumerate(chunks):
-        part = pl.ds((c * modes + lo) * tiles, (hi - lo) * tiles)
-        copies.append(pltpu.make_async_copy(basis_ref.at[part], buf.at[part], sems.at[i]))
+    for c in range(3):
+        part = pl.ds(c * size, size)
+        copies.append(pltpu.make_async_copy(basis_ref.at[part], buf.at[part], sems.at[c]))
     lists = pltpu.make_async_copy(send_hbm, send_ref, send_sem)
     lists.start()
     for copy in copies:
@@ -41,81 +41,85 @@
     lists.wait()
     for t in range(tiles):
         count = lax.broadcasted_iota(jnp.int32, (LANES, LANES), 0) + t * LANES
-        for side in range(2):
-            hot = jnp.broadcast_to(send_ref[2 + side], (LANES, LANES)) == count
-            hot_ref[t * LANES : (t + 1) * LANES, side * LANES : (side + 1) * LANES] = jnp.where(
-                hot, 1.0, 0.0
-            ).astype(jnp.bfloat16)
-    picks = []
-    for side in range(2):
-        nodes = jnp.broadcast_to(send_ref[side], (8, LANES))
-        picks.append((nodes & (LANES - 1), nodes >> 7))
-
-    def split(i):
-        c, lo, hi = chunks[i]
-        copies[i].wait()
-        for m in range(lo, hi, 16):
+        for side in range(4):
+            ref = hot_ref if side < 2 else hot_y
+            hot = jnp.broadcast_to(send_ref[side], (LANES, LANES)) == count
+            at = (side % 2) * LANES
+            ref[t * LANES : (t + 1) * LANES, at : at + LANES] = jnp.where(hot, 1.0, 0.0).astype(jnp.bfloat16)
+
+    def split(c):
+        copies[c].wait()
+        for m in range(c * modes, (c + 1) * modes, 16):
             for t in range(tiles):
-                at = (c * modes + m) * tiles + t
-                rows = [buf[pl.ds(at + 8 * tiles * h, 8, stride=tiles), :] for h in range(2)]
+                rows = [buf[pl.ds((m + 8 * h) * tiles + t, 8, stride=tiles), :] for h in range(2)]
                 rest = jnp.concatenate(rows, axis=0)
                 for s in range(PIECES):
                     piece = rest.astype(jnp.bfloat16)
-                    piece_ref[s, c * modes + m : c * modes + m + 16, t * LANES : (t + 1) * LANES] = piece
+                    piece_ref[s, m : m + 16, t * LANES : (t + 1) * LANES] = piece
                     if s + 1 < PIECES:
                         rest = rest - piece.astype(jnp.float32)
 
-    def pick(i):
-        c, lo, hi = chunks[i]
-        at = slice(c * modes + lo, c * modes + hi)
-        total = None
-        for s in range(PIECES):
-            part = jnp.dot(piece_ref[s, at, :], hot_ref[...], preferred_element_type=jnp.float32)
-            total = part if total is None else total + part
-        outs[2][at, :] = total[:, :LANES]
-        outs[3][at, :] = total[:, LANES:]
-
-    def permute(i):
-        c, lo, hi = chunks[i]
-        for m in range(c * modes + lo, c * modes + hi, 8):
-            sums = [jnp.zeros((8, LANES), jnp.float32) for _ in range(2)]
-            for t in range(tiles):
-                rows = buf[pl.ds(m * tiles + t, 8, stride=tiles), :]
-                for side, (lanes, tile) in enumerate(picks):
-                    sums[side] = jnp.where(tile == t, lane_pick(rows, lanes), sums[side])
-            for side in range(2):
-                outs[side][m : m + 8, :] = sums[side]
-
     split(0)
-    for i in range(len(chunks)):
-        permute(i)
-        pick(i)
-        if i + 1 < len(chunks):
-            split(i + 1)
+    for c in range(3):
+        if c < 2:
+            split(c + 1)
+        pick(c, modes, piece_ref, hot_y, below_ref, above_ref)
+
+
+def pick(c, modes, piece_ref, hot_ref, below_ref, above_ref):
+    at = slice(c * modes, (c + 1) * modes)
+    total = None
+    for s in range(PIECES):
+        part = jnp.dot(piece_ref[s, at, :], hot_ref[...], preferred_element_type=jnp.float32)
+        total = part if total is None else total + part
+    below_ref[at, :] = total[:, :LANES]
+    above_ref[at, :] = total[:, LANES:]
 
 
 def load(basis, send, modes):
     rows = basis.shape[0]
     tiles = rows // (3 * modes)
-    bounds = BOUNDS
     shared = jax.ShapeDtypeStruct((3 * modes, LANES), jnp.float32)
+    hot = (tiles * LANES, 2 * LANES)
     basis = pltpu.with_memory_space_constraint(basis, pltpu.HBM)
     send = pltpu.with_memory_space_constraint(send, pltpu.HBM)
     return pl.pallas_call(
-        functools.partial(load_kernel, modes, tiles, bounds),
-        out_shape=(jax.ShapeDtypeStruct(basis.shape, jnp.float32),) + (shared,) * 4,
+        functools.partial(load_kernel, modes, tiles),
+        out_shape=(
+            jax.ShapeDtypeStruct(basis.shape, jnp.float32),
+            jax.ShapeDtypeStruct((PIECES, 3 * modes, tiles * LANES), jnp.bfloat16),
+            jax.ShapeDtypeStruct(hot, jnp.bfloat16),
+            shared,
+            shared,
+        ),
         in_specs=[HBM, HBM],
         out_specs=(VMEM,) * 5,
         scratch_shapes=[
             pltpu.VMEM(send.shape, jnp.int32),
-            pltpu.VMEM((tiles * LANES, 2 * LANES), jnp.bfloat16),
-            pltpu.VMEM((PIECES, 3 * modes, tiles * LANES), jnp.bfloat16),
-            pltpu.SemaphoreType.DMA((3 * (len(bounds) - 1),)),
+            pltpu.VMEM(hot, jnp.bfloat16),
+            pltpu.SemaphoreType.DMA((3,)),
             pltpu.SemaphoreType.DMA,
         ],
-        compiler_params=pltpu.CompilerParams(vmem_limit_bytes=32 * MIB),
+        compiler_params=pltpu.CompilerParams(vmem_limit_bytes=24 * MIB),
         name="load",
     )(basis, send)
+
+
+def share_kernel(modes, piece_ref, hot_ref, below_ref, above_ref):
+    for c in range(3):
+        pick(c, modes, piece_ref, hot_ref, below_ref, above_ref)
+
+
+def share(pieces, hot, modes):
+    shared = jax.ShapeDtypeStruct((3 * modes, LANES), jnp.float32)
+    return pl.pallas_call(
+        functools.partial(share_kernel, modes),
+        out_shape=(shared, shared),
+        in_specs=[VMEM, VMEM],
+        out_specs=(VMEM,) * 2,
+        compiler_params=pltpu.CompilerParams(vmem_limit_bytes=16 * MIB),
+        name="share",
+    )(pieces, hot)
 
 
 def edges():
@@ -367,9 +371,10 @@
     coords, velocity, external = (x[None, :] for x in (coords, velocity, external))
     devices = lax.axis_size("gx") * lax.axis_size("gy")
 
-    dense, below_x, above_x, below_y, above_y = load(flat, send_nodes, modes)
-    r0, r1 = exchange(below_x, above_x, "gx")
-    r2, r3 = exchange(below_y, above_y, "gy")
+    dense, pieces, hot, below, above = load(flat, send_nodes, modes)
+    r2, r3 = exchange(below, above, "gy")
+    below, above = share(pieces, hot, modes)
+    r0, r1 = exchange(below, above, "gx")
     owned, low, high = prepare(dense, links, coords)
     sides = (r0, r1, r2, r3)
 

time: 73.4 us -> 74 us (level)
    pallas_call x1 -> x2, Pallas kernels: 5.7 us -> 6.31 us  [the longest x1 4.57 us: load(): pl.pallas_call(functools.partial(load_kernel, modes, tiles), out_shape=(j...]
where the time goes in v5:
time: 74 us; the launch traced here: 73.8 us
  blocking collectives  37.1 us (50%)
  Pallas kernels  16.3 us (22%)
  waiting for transfers between devices  10.9 us (15%)
  starting transfers between devices  8.64 us (12%)
  between operations  0.76 us (1%)
    all_to_all x2, blocking collectives, everyone(): lax.all_to_all(chunks, ('gx', 'gy'), 0, 0, tiled=True).reshape(parts.shape)  37.1 us
    ppermute x4, waiting for transfers between devices, exchange(): return (lax.ppermute(above, axis, up), lax.ppermute(below, axis, down))  10.9 us
    ppermute x4, starting transfers between devices, exchange(): return (lax.ppermute(above, axis, up), lax.ppermute(below, axis, down))  8.64 us
    pallas_call x2, Pallas kernels, step(): pl.pallas_call(functools.partial(step_kernel, first, modes, tiles), out_s...  7.07 us
    pallas_call x1, Pallas kernels, load(): pl.pallas_call(functools.partial(load_kernel, modes, tiles), out_shape=(j...  4.57 us
    pallas_call x1, Pallas kernels, share(): pl.pallas_call(functools.partial(share_kernel, modes), out_shape=(shared,...  1.74 us
    pallas_call x1, Pallas kernels, finish(): pl.pallas_call(functools.partial(final_kernel, modes, tiles), out_shape=(...  1.51 us
  transfers between devices with their start and end apart: 4, of which 2 were waited for; matrix products, arithmetic and copies ran while one was open for 0% of the time, Pallas kernels for 2%

profile of v5, /device:TPU:1, one launch (start us, length us, event | category | flops | bytes accessed | tf_op | source)
XLA Modules:
  0.0 73.8 jit_solution(10521697201512189175)
XLA Ops:
  0.6 0.0 copy-start.6
  0.6 0.0 copy-start.1
  0.7 4.6 %load.1 = (f32[12000,128]{1,0:T(8,128)S(1)}, bf16[2,1200,1280]{2,1,0:T(8,128)(2,1)S(1)}, bf16[1280,256]{1,0:T(8,128)(2,1)S(1)}, f32[1200,128]{1,0:T(8,128)S(1)}, f32[1200,128]{1,0:T(8,128)S(1)}) custom-call(f32[12000,128]{1,0:T(8,128)} %bitcast.27, s32[4,1,128]{2,1,0:T(1,128)} %send_hbm.1), custom_call_target="tpu_custom_call" | custom-call | tf_op jit(solution)/shard_map/load/pallas_call | solution.py:86
  5.2 0.0 copy-start
  5.2 0.0 copy-start.2
  5.3 0.0 copy-start.3
  5.3 1.7 %share.1 = (f32[1200,128]{1,0:T(8,128)S(1)}, f32[1200,128]{1,0:T(8,128)S(1)}) custom-call(bf16[2,1200,1280]{2,1,0:T(8,128)(2,1)S(1)} %get-tuple-element.23.piece_ref, bf16[1280,256]{1,0:T(8,128)(2,1)S(1)} %get-tuple-element.24.hot_ref), custom_call_target="tpu_custom_call" | custom-call | tf_op jit(solution)/shard_map/share/pallas_call | solution.py:115
  7.0 2.7 %collective-permute-start = (f32[1200,128]{1,0:T(8,128)S(1)}, f32[1200,128]{1,0:T(8,128)S(1)}, u32[]{:S(2)}, u32[]{:S(2)}) collective-permute-start(f32[1200,128]{1,0:T(8,128)S(1)} %get-tuple-element.25), channel_id=1, source_target_pairs={{0,16},{16,32},{32,48},{48,64},{64,80},{80,96},{96,112},{112,0},{1... | collective-permute-start | bytes 1843208 | tf_op jit(solution)/shard_map/ppermute | solution.py:358
  9.7 0.0 collective-permute-start.1
  9.7 1.2 %collective-permute-start.2 = (f32[1200,128]{1,0:T(8,128)S(1)}, f32[1200,128]{1,0:T(8,128)S(1)}, u32[]{:S(2)}, u32[]{:S(2)}) collective-permute-start(f32[1200,128]{1,0:T(8,128)S(1)} %get-tuple-element.27), channel_id=1, source_target_pairs={{0,1},{1,2},{2,3},{3,4},{4,5},{5,6},{6,7},{7,8},{8,9},{9,10},{10,1... | collective-permute-start | bytes 1843208 | tf_op jit(solution)/shard_map/ppermute | solution.py:358
  10.9 4.7 %collective-permute-start.3 = (f32[1200,128]{1,0:T(8,128)S(1)}, f32[1200,128]{1,0:T(8,128)S(1)}, u32[]{:S(2)}, u32[]{:S(2)}) collective-permute-start(f32[1200,128]{1,0:T(8,128)S(1)} %get-tuple-element.28), channel_id=1, source_target_pairs={{1,0},{2,1},{3,2},{4,3},{5,4},{6,5},{7,6},{8,7},{9,8},{10,9},{11,1... | collective-permute-start | bytes 1843208 | tf_op jit(solution)/shard_map/ppermute | solution.py:358
  15.7 0.0 copy-done.6
  15.7 0.0 copy-done.1
  15.7 1.5 %prepare.1 = (f32[32,128]{1,0:T(8,128)S(1)}, bf16[128,8192]{1,0:T(8,128)(2,1)S(1)}, bf16[16,8192]{1,0:T(8,128)(2,1)S(1)}) custom-call(f32[12000,128]{1,0:T(8,128)S(1)} %get-tuple-element.21.dense_ref.refs_1_, s32[8,1024]{1,0:T(8,128)S(1)} %bitcast.17, f32[1,400]{1,0:T(1,128)S(1)} %bitcast.21), custom_call_target="tpu_custom_call" | custom-call | tf_op jit(solution)/shard_map/prepare/pallas_call | solution.py:178
  17.1 0.0 copy-start.4
  17.2 0.0 copy-start.5
  17.2 0.0 collective-permute-done.refs_2_
  17.2 2.4 %collective-permute-done.1.refs_3_ = f32[1200,128]{1,0:T(8,128)S(1)} collective-permute-done((f32[1200,128]{1,0:T(8,128)S(1)}, f32[1200,128]{1,0:T(8,128)S(1)}, u32[]{:S(2)}, u32[]{:S(2)}) %collective-permute-start.1) | collective-permute-done | bytes 614432 | tf_op jit(solution)/shard_map/ppermute | solution.py:358
  19.6 8.5 %collective-permute-done.2.refs_4_ = f32[1200,128]{1,0:T(8,128)S(1)} collective-permute-done((f32[1200,128]{1,0:T(8,128)S(1)}, f32[1200,128]{1,0:T(8,128)S(1)}, u32[]{:S(2)}, u32[]{:S(2)}) %collective-permute-start.2) | collective-permute-done | bytes 614432 | tf_op jit(solution)/shard_map/ppermute | solution.py:358
  28.1 0.0 collective-permute-done.3.refs_5_
  28.1 0.0 copy-done
  28.1 0.0 copy-done.2
  28.1 0.0 copy-done.3
  28.1 3.2 %first_step.1 = f32[512,128]{1,0:T(8,128)S(1)} custom-call(f32[32,128]{1,0:T(8,128)S(1)} %get-tuple-element.22.refs_0_, f32[12000,128]{1,0:T(8,128)S(1)} %get-tuple-element.21.dense_ref.refs_1_, f32[1200,128]{1,0:T(8,128)S(1)} %collective-permute-done.refs_2_, f32[1200,128]{1,0:T(8,128)S(1)} %collective-permute-done.1.refs_3_, ...), custom_call_target="tpu_custom_call" | custom-call | tf_op jit(solution)/shard_map/first_step/pallas_call | solution.py:310
  31.4 21.9 %all_to_all.10 = f32[128,4,128]{2,1,0:T(4,128)S(1)} all-to-all(f32[128,4,128]{2,1,0:T(4,128)S(1)} %bitcast.16), channel_id=1, replica_groups=mesh['gx'=8,'gy'=16] {'gx','gy'}, dimensions={0} | all-to-all | bytes 524288 | tf_op jit(solution)/shard_map/all_to_all | solution.py:363
  53.2 0.0 copy-done.4
  53.2 0.0 copy-done.5
  53.2 3.9 %next_step.1 = (f32[512,128]{1,0:T(8,128)S(1)}, f32[1,400]{1,0:T(1,128)S(1)}, f32[1,400]{1,0:T(1,128)S(1)}) custom-call(f32[512,128]{1,0:T(8,128)S(1)} %bitcast.14, f32[12000,128]{1,0:T(8,128)S(1)} %get-tuple-element.21.dense_ref.refs_1_, f32[1200,128]{1,0:T(8,128)S(1)} %collective-permute-done.refs_2_, f32[1200,128]{1,0:T(8,128)S(1)} %collective-permute-done.1.refs_3_, ...), custom_call_target="tpu_custom_call" | custom-call | tf_op jit(solution)/shard_map/next_step/pallas_call | solution.py:310
  57.1 15.2 %all_to_all.11 = f32[128,4,128]{2,1,0:T(4,128)S(1)} all-to-all(f32[128,4,128]{2,1,0:T(4,128)S(1)} %bitcast.20), channel_id=1, replica_groups=mesh['gx'=8,'gy'=16] {'gx','gy'}, dimensions={0} | all-to-all | bytes 524288 | tf_op jit(solution)/shard_map/all_to_all | solution.py:363
  72.3 1.5 %finish.1 = (f32[1,400]{1,0:T(1,128)}, f32[1,400]{1,0:T(1,128)}, f32[1,400]{1,0:T(1,128)}, f32[3,1,1280]{2,1,0:T(1,128)}) custom-call(f32[512,128]{1,0:T(8,128)S(1)} %bitcast.15, f32[12000,128]{1,0:T(8,128)S(1)} %get-tuple-element.21.dense_ref.refs_1_, f32[1,400]{1,0:T(1,128)S(1)} %get-tuple-element.32.coords_ref, ...), custom_call_target="tpu_custom_call" | custom-call | tf_op jit(solution)/shard_map/finish/pallas_call | solution.py:343
  (1 shorter events, 0.0 us)
Async XLA Ops:
  0.6 15.0 %copy-start.6 = (s32[8,1,1024]{2,1,0:T(1,128)S(1)}, s32[8,1,1024]{2,1,0:T(1,128)}, u32[]{:S(2)}) copy-start(s32[8,1,1024]{2,1,0:T(1,128)} %param.10) | copy-start | bytes 98308
  0.6 15.0 %copy-start.1 = (f32[400]{0:T(512)S(1)}, f32[400]{0:T(512)}, u32[]{:S(2)}) copy-start(f32[400]{0:T(512)} %param.15) | copy-start | bytes 4804
  5.2 22.9 %copy-start = (f32[24,24]{1,0:T(8,128)S(1)}, f32[24,24]{1,0:T(8,128)}, u32[]{:S(2)}) copy-start(f32[24,24]{1,0:T(8,128)} %refs_11_.3) | copy-start | bytes 6916
  5.2 22.9 %copy-start.2 = (f32[1,1024]{1,0:T(1,128)S(1)}, f32[1,1024]{1,0:T(1,128)}, u32[]{:S(2)}) copy-start(f32[1,1024]{1,0:T(1,128)} %refs_9_.3) | copy-start | bytes 12292
  5.3 22.9 %copy-start.3 = (f32[1,1024]{1,0:T(1,128)S(1)}, f32[1,1024]{1,0:T(1,128)}, u32[]{:S(2)}) copy-start(f32[1,1024]{1,0:T(1,128)} %refs_10_.3) | copy-start | bytes 12292
  7.0 10.2 %collective-permute-start = (f32[1200,128]{1,0:T(8,128)S(1)}, f32[1200,128]{1,0:T(8,128)S(1)}, u32[]{:S(2)}, u32[]{:S(2)}) collective-permute-start(f32[1200,128]{1,0:T(8,128)S(1)} %get-tuple-element.25), channel_id=1, source_target_pairs={{0,16},{16,32},{32,48},{48,64},{64,80},{80,96},{96,112},{112,0},{1... | collective-permute-start | bytes 1843208 | tf_op jit(solution)/shard_map/ppermute | solution.py:358
  9.7 9.9 %collective-permute-start.1 = (f32[1200,128]{1,0:T(8,128)S(1)}, f32[1200,128]{1,0:T(8,128)S(1)}, u32[]{:S(2)}, u32[]{:S(2)}) collective-permute-start(f32[1200,128]{1,0:T(8,128)S(1)} %get-tuple-element.26), channel_id=1, source_target_pairs={{16,0},{32,16},{48,32},{64,48},{80,64},{96,80},{112,96},{0,112},{1... | collective-permute-start | bytes 1843208 | tf_op jit(solution)/shard_map/ppermute | solution.py:358
  9.7 18.4 %collective-permute-start.2 = (f32[1200,128]{1,0:T(8,128)S(1)}, f32[1200,128]{1,0:T(8,128)S(1)}, u32[]{:S(2)}, u32[]{:S(2)}) collective-permute-start(f32[1200,128]{1,0:T(8,128)S(1)} %get-tuple-element.27), channel_id=1, source_target_pairs={{0,1},{1,2},{2,3},{3,4},{4,5},{5,6},{6,7},{7,8},{8,9},{9,10},{10,1... | collective-permute-start | bytes 1843208 | tf_op jit(solution)/shard_map/ppermute | solution.py:358
  10.9 17.2 %collective-permute-start.3 = (f32[1200,128]{1,0:T(8,128)S(1)}, f32[1200,128]{1,0:T(8,128)S(1)}, u32[]{:S(2)}, u32[]{:S(2)}) collective-permute-start(f32[1200,128]{1,0:T(8,128)S(1)} %get-tuple-element.28), channel_id=1, source_target_pairs={{1,0},{2,1},{3,2},{4,3},{5,4},{6,5},{7,6},{8,7},{9,8},{10,9},{11,1... | collective-permute-start | bytes 1843208 | tf_op jit(solution)/shard_map/ppermute | solution.py:358
  17.1 36.1 %copy-start.4 = (f32[400]{0:T(512)S(1)}, f32[400]{0:T(512)}, u32[]{:S(2)}) copy-start(f32[400]{0:T(512)} %param.17) | copy-start | bytes 4804
  17.2 36.1 %copy-start.5 = (f32[400]{0:T(512)S(1)}, f32[400]{0:T(512)}, u32[]{:S(2)}) copy-start(f32[400]{0:T(512)} %param.16) | copy-start | bytes 4804
